TPU v7x, 128 devices: a whole 4x4x4 slice. The times are simulated.
128 devices in a mesh: stage: 2 (over core), data: 64 (over z, y, x).
Axes of the slice: x: 4, y: 4, z: 4, core: 2. Of those that a mesh axis runs over, the one named last changes fastest.
Arguments:
- x_in: bfloat16 [16, 4096, 1024], P(None, 'data')
- targets: bfloat16 [16, 4096, 1024], P(None, 'data')
- w_work: bfloat16 [2, 1, 8388608], P('stage')
- w_master: float32 [2, 1, 8388608], P('stage', None, 'data')
- m_prior: float32 [2, 1, 8388608], P('stage', None, 'data')
- v_prior: float32 [2, 1, 8388608], P('stage', None, 'data')
- clip_tau: float32 [], replicated
Outputs:
- output 1: float32 [], replicated
- output 2: bfloat16 [2, 1, 8388608], P('stage')
- output 3: float32 [2, 1, 8388608], P('stage', None, 'data')
- output 4: float32 [2, 1, 8388608], P('stage', None, 'data')
- output 5: float32 [2, 1, 8388608], P('stage', None, 'data')
All inputs are finite; a program needn't handle non-finite values.
Results may differ from a plain program's by a relative error of at most 0.001.
Values are sent between devices in bfloat16 or wider.
A program may use at most 1 GiB of HBM per device.

v0:
```python
import math
import jax
import jax.numpy as jnp
from jax import lax
from jax.sharding import PartitionSpec as P

ADAM_BETA1 = 0.9
ADAM_BETA2 = 0.95
ADAM_EPS = 1e-8
WEIGHT_DECAY = 0.1
ADAM_STEP = 10
LR_BASE = 0.05


def gelu_tanh(z_val):
    return jax.nn.gelu(z_val, approximate=True)


def split_layer(w_flat, d_model):
    half_len = 4 * d_model * d_model
    return w_flat[:half_len].reshape(d_model, 4 * d_model), w_flat[half_len:].reshape(4 * d_model, d_model)


def stage_forward(hidden, w_in_list, w_out_list):
    saved_in = []
    saved_pre = []
    for w_in, w_out in zip(w_in_list, w_out_list):
        pre_act = jnp.dot(hidden, w_in, preferred_element_type=jnp.float32).astype(jnp.bfloat16)
        act_bf = gelu_tanh(pre_act.astype(jnp.float32)).astype(jnp.bfloat16)
        saved_in.append(hidden)
        saved_pre.append(pre_act)
        hidden = (hidden.astype(jnp.float32) + jnp.dot(act_bf, w_out, preferred_element_type=jnp.float32)).astype(jnp.bfloat16)
    return hidden, jnp.stack(saved_in), jnp.stack(saved_pre)


def stage_backward(grad_h, saved_in, saved_pre, w_in_list, w_out_list, acc_in, acc_out):
    acc_in = list(acc_in)
    acc_out = list(acc_out)
    for layer_idx in reversed(range(len(w_in_list))):
        act_f, gelu_pull = jax.vjp(gelu_tanh, saved_pre[layer_idx].astype(jnp.float32))
        act_bf = act_f.astype(jnp.bfloat16)
        grad_act = jnp.einsum('nk,fk->nf', grad_h, w_out_list[layer_idx], preferred_element_type=jnp.float32)
        grad_pre = gelu_pull(grad_act)[0].astype(jnp.bfloat16)
        acc_out[layer_idx] = acc_out[layer_idx] + jnp.einsum('nf,nk->fk', act_bf, grad_h, preferred_element_type=jnp.float32)
        acc_in[layer_idx] = acc_in[layer_idx] + jnp.einsum('nk,nf->kf', saved_in[layer_idx], grad_pre, preferred_element_type=jnp.float32)
        grad_h = (grad_h.astype(jnp.float32) + jnp.einsum('nf,kf->nk', grad_pre, w_in_list[layer_idx], preferred_element_type=jnp.float32)).astype(jnp.bfloat16)
    return grad_h, acc_in, acc_out


def run_stages(x_in, targets, w_work, stages, data_size):
    micro_n, tok_rows, d_model = x_in.shape
    layers = w_work.shape[1]
    token_count = micro_n * tok_rows * data_size
    stage_idx = lax.axis_index('stage')
    is_first = stage_idx == 0
    is_last = stage_idx == stages - 1
    w_in_list = []
    w_out_list = []
    for layer_idx in range(layers):
        w_in, w_out = split_layer(w_work[0, layer_idx], d_model)
        w_in_list.append(w_in)
        w_out_list.append(w_out)
    stash_slots = min(micro_n, 2 * stages - 1)
    tick_count = micro_n + 2 * stages - 2
    fwd_pairs = [(src, src + 1) for src in range(stages - 1)]
    bwd_pairs = [(src + 1, src) for src in range(stages - 1)]

    def tick_body(tick_idx, loop_state):
        recv_act, recv_grad, stash_in, stash_pre, acc_in, acc_out, loss_acc = loop_state
        fwd_id = tick_idx - stage_idx
        fwd_ok = (fwd_id >= 0) & (fwd_id < micro_n)
        fwd_safe = jnp.clip(fwd_id, 0, micro_n - 1)
        first_rows = lax.dynamic_index_in_dim(x_in, fwd_safe, 0, keepdims=False)
        act_in = jnp.where(is_first, first_rows, recv_act)

        def run_fwd(hidden):
            return stage_forward(hidden, w_in_list, w_out_list)

        def skip_fwd(hidden):
            return hidden, jnp.zeros((layers, tok_rows, d_model), jnp.bfloat16), jnp.zeros((layers, tok_rows, 4 * d_model), jnp.bfloat16)

        act_out, new_in, new_pre = lax.cond(fwd_ok, run_fwd, skip_fwd, act_in)
        write_slot = jnp.where(fwd_ok, fwd_safe % stash_slots, stash_slots)
        stash_in = lax.dynamic_update_index_in_dim(stash_in, new_in, write_slot, 0)
        stash_pre = lax.dynamic_update_index_in_dim(stash_pre, new_pre, write_slot, 0)
        target_rows = lax.dynamic_index_in_dim(targets, fwd_safe, 0, keepdims=False)
        residual = act_out.astype(jnp.float32) - target_rows.astype(jnp.float32)
        loss_acc = loss_acc + jnp.where(fwd_ok & is_last, 0.5 * jnp.sum(residual * residual), 0.0)
        top_grad = (residual / token_count).astype(jnp.bfloat16)
        bwd_id = tick_idx - (2 * stages - 2 - stage_idx)
        bwd_ok = (bwd_id >= 0) & (bwd_id < micro_n)
        read_slot = jnp.clip(bwd_id, 0, micro_n - 1) % stash_slots
        held_in = lax.dynamic_index_in_dim(stash_in, read_slot, 0, keepdims=False)
        held_pre = lax.dynamic_index_in_dim(stash_pre, read_slot, 0, keepdims=False)
        grad_in = jnp.where(is_last, top_grad, recv_grad)

        def run_bwd(bwd_args):
            return stage_backward(bwd_args[0], held_in, held_pre, w_in_list, w_out_list, bwd_args[1], bwd_args[2])

        def skip_bwd(bwd_args):
            return bwd_args

        grad_out, acc_in, acc_out = lax.cond(bwd_ok, run_bwd, skip_bwd, (grad_in, acc_in, acc_out))
        recv_act = lax.ppermute(act_out, 'stage', fwd_pairs)
        recv_grad = lax.ppermute(grad_out, 'stage', bwd_pairs)
        return (recv_act, recv_grad, stash_in, stash_pre, acc_in, acc_out, loss_acc)

    start_state = (
        jnp.zeros((tok_rows, d_model), jnp.bfloat16),
        jnp.zeros((tok_rows, d_model), jnp.bfloat16),
        jnp.zeros((stash_slots + 1, layers, tok_rows, d_model), jnp.bfloat16),
        jnp.zeros((stash_slots + 1, layers, tok_rows, 4 * d_model), jnp.bfloat16),
        [jnp.zeros((d_model, 4 * d_model), jnp.float32) for _ in range(layers)],
        [jnp.zeros((4 * d_model, d_model), jnp.float32) for _ in range(layers)],
        jnp.zeros((), jnp.float32),
    )
    end_state = lax.fori_loop(0, tick_count, tick_body, start_state)
    acc_in = end_state[4]
    acc_out = end_state[5]
    grad_local = jnp.stack([jnp.concatenate([acc_in[layer_idx].reshape(-1), acc_out[layer_idx].reshape(-1)]) for layer_idx in range(layers)])[None]
    return grad_local, end_state[6], token_count


def adam_update(w_master, m_prior, v_prior, grad_part, clip_scale, d_model):
    scaled = clip_scale * grad_part
    m_new = ADAM_BETA1 * m_prior + (1.0 - ADAM_BETA1) * scaled
    v_new = ADAM_BETA2 * v_prior + (1.0 - ADAM_BETA2) * scaled * scaled
    m_hat = m_new / (1.0 - ADAM_BETA1 ** ADAM_STEP)
    v_hat = v_new / (1.0 - ADAM_BETA2 ** ADAM_STEP)
    learn_rate = LR_BASE / math.sqrt(d_model)
    w_new = w_master - learn_rate * (m_hat / (jnp.sqrt(v_hat) + ADAM_EPS) + WEIGHT_DECAY * w_master)
    return w_new, m_new, v_new


def solution(mesh):
    stages = mesh.shape['stage']
    data_size = mesh.shape['data']

    def device_step(x_in, targets, w_work, w_master, m_prior, v_prior, clip_tau):
        grad_local, loss_acc, token_count = run_stages(x_in, targets, w_work, stages, data_size)
        grad_part = lax.psum_scatter(grad_local, 'data', scatter_dimension=2, tiled=True)
        sq_total = lax.psum(jnp.sum(grad_part * grad_part), ('stage', 'data'))
        clip_scale = jnp.minimum(1.0, clip_tau / jnp.sqrt(sq_total))
        w_new, m_new, v_new = adam_update(w_master, m_prior, v_prior, grad_part, clip_scale, x_in.shape[-1])
        w_bf16 = lax.all_gather(w_new.astype(jnp.bfloat16), 'data', axis=2, tiled=True)
        loss_mean = lax.psum(loss_acc, ('stage', 'data')) / token_count
        return loss_mean, w_bf16, w_new, m_new, v_new

    row_spec = P(None, 'data', None)
    shard_spec = P('stage', None, 'data')
    stage_spec = P('stage', None, None)
    return jax.shard_map(device_step, mesh=mesh, in_specs=(row_spec, row_spec, stage_spec, shard_spec, shard_spec, shard_spec, P()), out_specs=(P(), stage_spec, shard_spec, shard_spec, shard_spec), check_vma=False)
```

profile of v0, /device:TPU:0, one launch (start us, length us, event | category | flops | bytes accessed | tf_op | source)
XLA Modules:
  0.0 1855.9 jit_solution(10129484219767480793)
XLA Ops:
  7.2 184.3 %slice_reduce_fusion = (bf16[4194304]{0:T(1024)(128)(2,1)}, bf16[4194304]{0:T(1024)(128)(2,1)}) fusion(bf16[1,1,8388608]{2,1,0:T(2,128)(2,1)} %param.15), kind=kLoop, calls=%fused_computation.62 | loop fusion | bytes 33554432 | tf_op jit(solution)/shard_map/slice | solution.py:21
  191.6 13.4 reshape.36
  204.9 13.3 reshape.37
  234.7 954.3 %while.27 = (s32[]{:T(128)}, bf16[64,1024]{1,0:T(8,128)(2,1)S(1)}, bf16[64,1024]{1,0:T(8,128)(2,1)S(1)}, bf16[4,1,64,1024]{3,2,1,0:T(8,128)(2,1)S(1)}, bf16[4,1,...) while((s32[]{:T(128)}, bf16[64,1024]{1,0:T(8,128)(2,1)S(1)}, ...), condition=%wide.region_6.7_spmd, body=%wide.region_0.6_spmd.sunk | while | flops 3247308800 | bytes 161351584 | solution.py:117
  254.2 8.6 conditional.4
  266.2 38.7 %collective-permute-start = (bf16[64,1024]{1,0:T(8,128)(2,1)S(1)}, bf16[64,1024]{1,0:T(8,128)(2,1)S(1)}, u32[]{:S(2)}, u32[]{:S(2)}) collective-permute-start(bf16[64,1024]{1,0:T(8,128)(2,1)S(1)} %get-tuple-element.699), channel_id=1, source_target_pairs={{0,64},{1,65},{2,66},{3,67},{4,68},{5,69},{6,70},{7,71},{8,72},{9,... | collective-permute-start | bytes 393224 | tf_op jit(solution)/shard_map/while/body/eval_jaxpr/ppermute | solution.py:104
  308.1 8.6 conditional.4
  318.8 37.4 %conditional.5 = ((bf16[64,1024]{1,0:T(8,128)(2,1)S(1)}, f32[1024,4096]{1,0:T(8,128)}, f32[4096,1024]{1,0:T(8,128)})) conditional(s32[]{:T(128)} %convert_element_type.167, (bf16[64,1024]{1,0:T(8,128)(2,1)S(1)}, f32[1024,4096]{1,0:T(8,128)}, f32[4096,1024]{1,0:T(8,128)}) %tuple.86, (bf16[64,1024]{1,0:T(8,128)(2,1)S(1)}, bf16[4096,1024]{1,0:T(8,128)(2,1)}, ...), branch_computations={%region_3.3_spmd, %region_4.4_spmd} | conditional | flops 2169700352 | bytes 114427072 | solution.py:103
  324.9 14.5 convolution_add_fusion.2
  339.4 14.0 convolution_add_fusion.1
  374.5 37.4 %conditional.5 = ((bf16[64,1024]{1,0:T(8,128)(2,1)S(1)}, f32[1024,4096]{1,0:T(8,128)}, f32[4096,1024]{1,0:T(8,128)})) conditional(s32[]{:T(128)} %convert_element_type.167, (bf16[64,1024]{1,0:T(8,128)(2,1)S(1)}, f32[1024,4096]{1,0:T(8,128)}, f32[4096,1024]{1,0:T(8,128)}) %tuple.86, (bf16[64,1024]{1,0:T(8,128)(2,1)S(1)}, bf16[4096,1024]{1,0:T(8,128)(2,1)}, ...), branch_computations={%region_3.3_spmd, %region_4.4_spmd} | conditional | flops 2169700352 | bytes 114427072 | solution.py:103
  380.6 14.5 convolution_add_fusion.2
  395.1 14.0 convolution_add_fusion.1
  430.2 37.4 %conditional.5 = ((bf16[64,1024]{1,0:T(8,128)(2,1)S(1)}, f32[1024,4096]{1,0:T(8,128)}, f32[4096,1024]{1,0:T(8,128)})) conditional(s32[]{:T(128)} %convert_element_type.167, (bf16[64,1024]{1,0:T(8,128)(2,1)S(1)}, f32[1024,4096]{1,0:T(8,128)}, f32[4096,1024]{1,0:T(8,128)}) %tuple.86, (bf16[64,1024]{1,0:T(8,128)(2,1)S(1)}, bf16[4096,1024]{1,0:T(8,128)(2,1)}, ...), branch_computations={%region_3.3_spmd, %region_4.4_spmd} | conditional | flops 2169700352 | bytes 114427072 | solution.py:103
  436.3 14.5 convolution_add_fusion.2
  450.8 14.0 convolution_add_fusion.1
  485.9 37.4 %conditional.5 = ((bf16[64,1024]{1,0:T(8,128)(2,1)S(1)}, f32[1024,4096]{1,0:T(8,128)}, f32[4096,1024]{1,0:T(8,128)})) conditional(s32[]{:T(128)} %convert_element_type.167, (bf16[64,1024]{1,0:T(8,128)(2,1)S(1)}, f32[1024,4096]{1,0:T(8,128)}, f32[4096,1024]{1,0:T(8,128)}) %tuple.86, (bf16[64,1024]{1,0:T(8,128)(2,1)S(1)}, bf16[4096,1024]{1,0:T(8,128)(2,1)}, ...), branch_computations={%region_3.3_spmd, %region_4.4_spmd} | conditional | flops 2169700352 | bytes 114427072 | solution.py:103
  492.0 14.5 convolution_add_fusion.2
  506.5 14.0 convolution_add_fusion.1
  541.6 37.4 %conditional.5 = ((bf16[64,1024]{1,0:T(8,128)(2,1)S(1)}, f32[1024,4096]{1,0:T(8,128)}, f32[4096,1024]{1,0:T(8,128)})) conditional(s32[]{:T(128)} %convert_element_type.167, (bf16[64,1024]{1,0:T(8,128)(2,1)S(1)}, f32[1024,4096]{1,0:T(8,128)}, f32[4096,1024]{1,0:T(8,128)}) %tuple.86, (bf16[64,1024]{1,0:T(8,128)(2,1)S(1)}, bf16[4096,1024]{1,0:T(8,128)(2,1)}, ...), branch_computations={%region_3.3_spmd, %region_4.4_spmd} | conditional | flops 2169700352 | bytes 114427072 | solution.py:103
  547.7 14.5 convolution_add_fusion.2
  562.3 14.0 convolution_add_fusion.1
  597.3 37.4 %conditional.5 = ((bf16[64,1024]{1,0:T(8,128)(2,1)S(1)}, f32[1024,4096]{1,0:T(8,128)}, f32[4096,1024]{1,0:T(8,128)})) conditional(s32[]{:T(128)} %convert_element_type.167, (bf16[64,1024]{1,0:T(8,128)(2,1)S(1)}, f32[1024,4096]{1,0:T(8,128)}, f32[4096,1024]{1,0:T(8,128)}) %tuple.86, (bf16[64,1024]{1,0:T(8,128)(2,1)S(1)}, bf16[4096,1024]{1,0:T(8,128)(2,1)}, ...), branch_computations={%region_3.3_spmd, %region_4.4_spmd} | conditional | flops 2169700352 | bytes 114427072 | solution.py:103
  603.4 14.5 convolution_add_fusion.2
  618.0 14.0 convolution_add_fusion.1
  642.4 8.6 conditional.4
  653.0 37.4 %conditional.5 = ((bf16[64,1024]{1,0:T(8,128)(2,1)S(1)}, f32[1024,4096]{1,0:T(8,128)}, f32[4096,1024]{1,0:T(8,128)})) conditional(s32[]{:T(128)} %convert_element_type.167, (bf16[64,1024]{1,0:T(8,128)(2,1)S(1)}, f32[1024,4096]{1,0:T(8,128)}, f32[4096,1024]{1,0:T(8,128)}) %tuple.86, (bf16[64,1024]{1,0:T(8,128)(2,1)S(1)}, bf16[4096,1024]{1,0:T(8,128)(2,1)}, ...), branch_computations={%region_3.3_spmd, %region_4.4_spmd} | conditional | flops 2169700352 | bytes 114427072 | solution.py:103
  659.1 14.5 convolution_add_fusion.2
  673.7 14.0 convolution_add_fusion.1
  708.7 37.4 %conditional.5 = ((bf16[64,1024]{1,0:T(8,128)(2,1)S(1)}, f32[1024,4096]{1,0:T(8,128)}, f32[4096,1024]{1,0:T(8,128)})) conditional(s32[]{:T(128)} %convert_element_type.167, (bf16[64,1024]{1,0:T(8,128)(2,1)S(1)}, f32[1024,4096]{1,0:T(8,128)}, f32[4096,1024]{1,0:T(8,128)}) %tuple.86, (bf16[64,1024]{1,0:T(8,128)(2,1)S(1)}, bf16[4096,1024]{1,0:T(8,128)(2,1)}, ...), branch_computations={%region_3.3_spmd, %region_4.4_spmd} | conditional | flops 2169700352 | bytes 114427072 | solution.py:103
  714.8 14.5 convolution_add_fusion.2
  729.4 14.0 convolution_add_fusion.1
  764.5 37.4 %conditional.5 = ((bf16[64,1024]{1,0:T(8,128)(2,1)S(1)}, f32[1024,4096]{1,0:T(8,128)}, f32[4096,1024]{1,0:T(8,128)})) conditional(s32[]{:T(128)} %convert_element_type.167, (bf16[64,1024]{1,0:T(8,128)(2,1)S(1)}, f32[1024,4096]{1,0:T(8,128)}, f32[4096,1024]{1,0:T(8,128)}) %tuple.86, (bf16[64,1024]{1,0:T(8,128)(2,1)S(1)}, bf16[4096,1024]{1,0:T(8,128)(2,1)}, ...), branch_computations={%region_3.3_spmd, %region_4.4_spmd} | conditional | flops 2169700352 | bytes 114427072 | solution.py:103
  770.5 14.5 convolution_add_fusion.2
  785.1 14.0 convolution_add_fusion.1
  820.2 37.4 %conditional.5 = ((bf16[64,1024]{1,0:T(8,128)(2,1)S(1)}, f32[1024,4096]{1,0:T(8,128)}, f32[4096,1024]{1,0:T(8,128)})) conditional(s32[]{:T(128)} %convert_element_type.167, (bf16[64,1024]{1,0:T(8,128)(2,1)S(1)}, f32[1024,4096]{1,0:T(8,128)}, f32[4096,1024]{1,0:T(8,128)}) %tuple.86, (bf16[64,1024]{1,0:T(8,128)(2,1)S(1)}, bf16[4096,1024]{1,0:T(8,128)(2,1)}, ...), branch_computations={%region_3.3_spmd, %region_4.4_spmd} | conditional | flops 2169700352 | bytes 114427072 | solution.py:103
  826.2 14.5 convolution_add_fusion.2
  840.8 14.0 convolution_add_fusion.1
  875.9 37.4 %conditional.5 = ((bf16[64,1024]{1,0:T(8,128)(2,1)S(1)}, f32[1024,4096]{1,0:T(8,128)}, f32[4096,1024]{1,0:T(8,128)})) conditional(s32[]{:T(128)} %convert_element_type.167, (bf16[64,1024]{1,0:T(8,128)(2,1)S(1)}, f32[1024,4096]{1,0:T(8,128)}, f32[4096,1024]{1,0:T(8,128)}) %tuple.86, (bf16[64,1024]{1,0:T(8,128)(2,1)S(1)}, bf16[4096,1024]{1,0:T(8,128)(2,1)}, ...), branch_computations={%region_3.3_spmd, %region_4.4_spmd} | conditional | flops 2169700352 | bytes 114427072 | solution.py:103
  881.9 14.5 convolution_add_fusion.2
  896.5 14.0 convolution_add_fusion.1
  931.6 37.4 %conditional.5 = ((bf16[64,1024]{1,0:T(8,128)(2,1)S(1)}, f32[1024,4096]{1,0:T(8,128)}, f32[4096,1024]{1,0:T(8,128)})) conditional(s32[]{:T(128)} %convert_element_type.167, (bf16[64,1024]{1,0:T(8,128)(2,1)S(1)}, f32[1024,4096]{1,0:T(8,128)}, f32[4096,1024]{1,0:T(8,128)}) %tuple.86, (bf16[64,1024]{1,0:T(8,128)(2,1)S(1)}, bf16[4096,1024]{1,0:T(8,128)(2,1)}, ...), branch_computations={%region_3.3_spmd, %region_4.4_spmd} | conditional | flops 2169700352 | bytes 114427072 | solution.py:103
  937.6 14.5 convolution_add_fusion.2
  952.2 14.0 convolution_add_fusion.1
  987.3 37.4 %conditional.5 = ((bf16[64,1024]{1,0:T(8,128)(2,1)S(1)}, f32[1024,4096]{1,0:T(8,128)}, f32[4096,1024]{1,0:T(8,128)})) conditional(s32[]{:T(128)} %convert_element_type.167, (bf16[64,1024]{1,0:T(8,128)(2,1)S(1)}, f32[1024,4096]{1,0:T(8,128)}, f32[4096,1024]{1,0:T(8,128)}) %tuple.86, (bf16[64,1024]{1,0:T(8,128)(2,1)S(1)}, bf16[4096,1024]{1,0:T(8,128)(2,1)}, ...), branch_computations={%region_3.3_spmd, %region_4.4_spmd} | conditional | flops 2169700352 | bytes 114427072 | solution.py:103
  993.4 14.5 convolution_add_fusion.2
  1007.9 14.0 convolution_add_fusion.1
  1043.0 37.4 %conditional.5 = ((bf16[64,1024]{1,0:T(8,128)(2,1)S(1)}, f32[1024,4096]{1,0:T(8,128)}, f32[4096,1024]{1,0:T(8,128)})) conditional(s32[]{:T(128)} %convert_element_type.167, (bf16[64,1024]{1,0:T(8,128)(2,1)S(1)}, f32[1024,4096]{1,0:T(8,128)}, f32[4096,1024]{1,0:T(8,128)}) %tuple.86, (bf16[64,1024]{1,0:T(8,128)(2,1)S(1)}, bf16[4096,1024]{1,0:T(8,128)(2,1)}, ...), branch_computations={%region_3.3_spmd, %region_4.4_spmd} | conditional | flops 2169700352 | bytes 114427072 | solution.py:103
  1049.1 14.5 convolution_add_fusion.2
  1063.6 14.0 convolution_add_fusion.1
  1091.0 37.4 %conditional.5 = ((bf16[64,1024]{1,0:T(8,128)(2,1)S(1)}, f32[1024,4096]{1,0:T(8,128)}, f32[4096,1024]{1,0:T(8,128)})) conditional(s32[]{:T(128)} %convert_element_type.167, (bf16[64,1024]{1,0:T(8,128)(2,1)S(1)}, f32[1024,4096]{1,0:T(8,128)}, f32[4096,1024]{1,0:T(8,128)}) %tuple.86, (bf16[64,1024]{1,0:T(8,128)(2,1)S(1)}, bf16[4096,1024]{1,0:T(8,128)(2,1)}, ...), branch_computations={%region_3.3_spmd, %region_4.4_spmd} | conditional | flops 2169700352 | bytes 114427072 | solution.py:103
  1097.0 14.5 convolution_add_fusion.2
  1111.6 14.0 convolution_add_fusion.1
  1129.7 9.0 collective-permute-start
  1144.9 37.4 %conditional.5 = ((bf16[64,1024]{1,0:T(8,128)(2,1)S(1)}, f32[1024,4096]{1,0:T(8,128)}, f32[4096,1024]{1,0:T(8,128)})) conditional(s32[]{:T(128)} %convert_element_type.167, (bf16[64,1024]{1,0:T(8,128)(2,1)S(1)}, f32[1024,4096]{1,0:T(8,128)}, f32[4096,1024]{1,0:T(8,128)}) %tuple.86, (bf16[64,1024]{1,0:T(8,128)(2,1)S(1)}, bf16[4096,1024]{1,0:T(8,128)(2,1)}, ...), branch_computations={%region_3.3_spmd, %region_4.4_spmd} | conditional | flops 2169700352 | bytes 114427072 | solution.py:103
  1151.0 14.5 convolution_add_fusion.2
  1165.5 14.0 convolution_add_fusion.1
  1189.0 14.3 copy.14
  1203.3 14.1 copy.15
  1217.4 24.8 %pad_maximum_fusion = f32[8388608]{0:T(1024)} fusion(f32[4194304]{0:T(1024)} %bitcast.49, f32[4194304]{0:T(1024)} %bitcast.48), kind=kLoop, calls=%fused_computation.61 | loop fusion | flops 8388608 | bytes 67108864 | tf_op jit(solution)/shard_map/concatenate | solution.py:120
  1244.2 335.8 %all-reduce.4.cloned.1.call-done = f32[1,1,8388608]{2,1,0:T(1,128)} async-done(((f32[1,1,8388608]{2,1,0:T(1,128)}), f32[1,1,8388608]{2,1,0:T(1,128)}) %all-reduce.4.cloned.1.call-update) | async-done | bytes 33554448
  1582.7 63.1 %all-reduce.1 = (f32[]{:T(128)}, f32[]{:T(128)}) all-reduce(f32[]{:T(128)} %get-tuple-element.553, f32[]{:T(128)} %multiply_reduce_fusion.1), channel_id=1, replica_groups=mesh['stage'=2,'data'=64] {'stage','data'}, use_global_device_ids=true, to_apply=%region_7.8 | all-reduce | flops 2 | bytes 16 | tf_op jit(solution)/shard_map/psum | solution.py:146
  1653.0 157.1 %all-gather.2.cloned.1.call-done = bf16[1,1,8388608]{2,1,0:T(2,128)(2,1)} async-done(((bf16[1,1,131072]{2,1,0:T(2,128)(2,1)}), bf16[1,1,8388608]{2,1,0:T(2,128)(2,1)}) %all-gather.2.cloned.1.call-update) | async-done | bytes 16777232 | tf_op jit(solution)/shard_map/all_gather | solution.py:145
  1810.1 37.8 %copy.57 = bf16[1,1,8388608]{2,1,0:T(2,128)(2,1)} copy(bf16[1,1,8388608]{2,1,0:T(2,128)(2,1)} %all-gather.2.cloned.1.call-done) | data formatting | bytes 33554432
  (428 shorter events, 572.7 us)
Async XLA Ops:
  7.2 1572.9 %all-reduce.4.cloned.1.call-start = ((), (), s32[]{:S(2)}) async-start(), calls=%async_computation.1 | async-start | bytes 67108864
  246.6 6.6 collective-permute-start.1
  247.9 5.3 collective-permute-start
  264.9 42.3 %collective-permute-start.1 = (bf16[64,1024]{1,0:T(8,128)(2,1)S(1)}, bf16[64,1024]{1,0:T(8,128)(2,1)S(1)}, u32[]{:S(2)}, u32[]{:S(2)}) collective-permute-start(bf16[64,1024]{1,0:T(8,128)(2,1)S(1)} %get-tuple-element.702), channel_id=1, source_target_pairs={{64,0},{65,1},{66,2},{67,3},{68,4},{69,5},{70,6},{71,7},{72,8},{73... | collective-permute-start | bytes 393224 | tf_op jit(solution)/shard_map/while/body/eval_jaxpr/ppermute | solution.py:105
  266.2 41.0 %collective-permute-start = (bf16[64,1024]{1,0:T(8,128)(2,1)S(1)}, bf16[64,1024]{1,0:T(8,128)(2,1)S(1)}, u32[]{:S(2)}, u32[]{:S(2)}) collective-permute-start(bf16[64,1024]{1,0:T(8,128)(2,1)S(1)} %get-tuple-element.699), channel_id=1, source_target_pairs={{0,64},{1,65},{2,66},{3,67},{4,68},{5,69},{6,70},{7,71},{8,72},{9,... | collective-permute-start | bytes 393224 | tf_op jit(solution)/shard_map/while/body/eval_jaxpr/ppermute | solution.py:104
  324.9 28.6 %slice-start.2 = ((s8[8388608]{0:T(1024)(128)(4,1)}), s8[4194304]{0:T(1024)(128)(4,1)S(1)}, s32[]{:S(2)}) async-start(s8[8388608]{0:T(1024)(128)(4,1)} %bitcast.44), calls=%async_computation.4 | async-start | bytes 8388608 | tf_op jit(solution)/shard_map/while/body/eval_jaxpr/cond
  339.4 14.0 slice-start.3
  356.2 6.6 collective-permute-start.1
  357.5 5.3 collective-permute-start
  380.6 28.6 %slice-start.2 = ((s8[8388608]{0:T(1024)(128)(4,1)}), s8[4194304]{0:T(1024)(128)(4,1)S(1)}, s32[]{:S(2)}) async-start(s8[8388608]{0:T(1024)(128)(4,1)} %bitcast.44), calls=%async_computation.4 | async-start | bytes 8388608 | tf_op jit(solution)/shard_map/while/body/eval_jaxpr/cond
  395.1 14.0 slice-start.3
  411.9 6.6 collective-permute-start.1
  413.2 5.3 collective-permute-start
  436.3 28.6 %slice-start.2 = ((s8[8388608]{0:T(1024)(128)(4,1)}), s8[4194304]{0:T(1024)(128)(4,1)S(1)}, s32[]{:S(2)}) async-start(s8[8388608]{0:T(1024)(128)(4,1)} %bitcast.44), calls=%async_computation.4 | async-start | bytes 8388608 | tf_op jit(solution)/shard_map/while/body/eval_jaxpr/cond
  450.8 14.0 slice-start.3
  467.6 6.6 collective-permute-start.1
  468.9 5.3 collective-permute-start
  492.0 28.6 %slice-start.2 = ((s8[8388608]{0:T(1024)(128)(4,1)}), s8[4194304]{0:T(1024)(128)(4,1)S(1)}, s32[]{:S(2)}) async-start(s8[8388608]{0:T(1024)(128)(4,1)} %bitcast.44), calls=%async_computation.4 | async-start | bytes 8388608 | tf_op jit(solution)/shard_map/while/body/eval_jaxpr/cond
  506.5 14.0 slice-start.3
  523.3 6.6 collective-permute-start.1
  524.6 5.3 collective-permute-start
  547.7 28.6 %slice-start.2 = ((s8[8388608]{0:T(1024)(128)(4,1)}), s8[4194304]{0:T(1024)(128)(4,1)S(1)}, s32[]{:S(2)}) async-start(s8[8388608]{0:T(1024)(128)(4,1)} %bitcast.44), calls=%async_computation.4 | async-start | bytes 8388608 | tf_op jit(solution)/shard_map/while/body/eval_jaxpr/cond
  562.3 14.0 slice-start.3
  579.1 6.6 collective-permute-start.1
  580.4 5.3 collective-permute-start
  603.4 28.6 %slice-start.2 = ((s8[8388608]{0:T(1024)(128)(4,1)}), s8[4194304]{0:T(1024)(128)(4,1)S(1)}, s32[]{:S(2)}) async-start(s8[8388608]{0:T(1024)(128)(4,1)} %bitcast.44), calls=%async_computation.4 | async-start | bytes 8388608 | tf_op jit(solution)/shard_map/while/body/eval_jaxpr/cond
  634.8 6.6 collective-permute-start.1
  636.1 5.3 collective-permute-start
  659.1 28.6 %slice-start.2 = ((s8[8388608]{0:T(1024)(128)(4,1)}), s8[4194304]{0:T(1024)(128)(4,1)S(1)}, s32[]{:S(2)}) async-start(s8[8388608]{0:T(1024)(128)(4,1)} %bitcast.44), calls=%async_computation.4 | async-start | bytes 8388608 | tf_op jit(solution)/shard_map/while/body/eval_jaxpr/cond
  690.5 6.6 collective-permute-start.1
  691.8 5.3 collective-permute-start
  714.8 28.6 %slice-start.2 = ((s8[8388608]{0:T(1024)(128)(4,1)}), s8[4194304]{0:T(1024)(128)(4,1)S(1)}, s32[]{:S(2)}) async-start(s8[8388608]{0:T(1024)(128)(4,1)} %bitcast.44), calls=%async_computation.4 | async-start | bytes 8388608 | tf_op jit(solution)/shard_map/while/body/eval_jaxpr/cond
  746.2 6.6 collective-permute-start.1
  747.5 5.3 collective-permute-start
  770.5 28.6 %slice-start.2 = ((s8[8388608]{0:T(1024)(128)(4,1)}), s8[4194304]{0:T(1024)(128)(4,1)S(1)}, s32[]{:S(2)}) async-start(s8[8388608]{0:T(1024)(128)(4,1)} %bitcast.44), calls=%async_computation.4 | async-start | bytes 8388608 | tf_op jit(solution)/shard_map/while/body/eval_jaxpr/cond
  801.9 6.6 collective-permute-start.1
  803.2 5.3 collective-permute-start
  826.2 28.6 %slice-start.2 = ((s8[8388608]{0:T(1024)(128)(4,1)}), s8[4194304]{0:T(1024)(128)(4,1)S(1)}, s32[]{:S(2)}) async-start(s8[8388608]{0:T(1024)(128)(4,1)} %bitcast.44), calls=%async_computation.4 | async-start | bytes 8388608 | tf_op jit(solution)/shard_map/while/body/eval_jaxpr/cond
  840.8 14.0 slice-start.3
  857.6 6.6 collective-permute-start.1
  858.9 5.3 collective-permute-start
  881.9 28.6 %slice-start.2 = ((s8[8388608]{0:T(1024)(128)(4,1)}), s8[4194304]{0:T(1024)(128)(4,1)S(1)}, s32[]{:S(2)}) async-start(s8[8388608]{0:T(1024)(128)(4,1)} %bitcast.44), calls=%async_computation.4 | async-start | bytes 8388608 | tf_op jit(solution)/shard_map/while/body/eval_jaxpr/cond
  896.5 14.0 slice-start.3
  913.3 6.6 collective-permute-start.1
  914.6 5.3 collective-permute-start
  937.6 28.6 %slice-start.2 = ((s8[8388608]{0:T(1024)(128)(4,1)}), s8[4194304]{0:T(1024)(128)(4,1)S(1)}, s32[]{:S(2)}) async-start(s8[8388608]{0:T(1024)(128)(4,1)} %bitcast.44), calls=%async_computation.4 | async-start | bytes 8388608 | tf_op jit(solution)/shard_map/while/body/eval_jaxpr/cond
  969.0 6.6 collective-permute-start.1
  970.3 5.3 collective-permute-start
  993.3 28.6 %slice-start.2 = ((s8[8388608]{0:T(1024)(128)(4,1)}), s8[4194304]{0:T(1024)(128)(4,1)S(1)}, s32[]{:S(2)}) async-start(s8[8388608]{0:T(1024)(128)(4,1)} %bitcast.44), calls=%async_computation.4 | async-start | bytes 8388608 | tf_op jit(solution)/shard_map/while/body/eval_jaxpr/cond
  1024.7 6.6 collective-permute-start.1
  1026.0 5.3 collective-permute-start
  1049.0 28.6 %slice-start.2 = ((s8[8388608]{0:T(1024)(128)(4,1)}), s8[4194304]{0:T(1024)(128)(4,1)S(1)}, s32[]{:S(2)}) async-start(s8[8388608]{0:T(1024)(128)(4,1)} %bitcast.44), calls=%async_computation.4 | async-start | bytes 8388608 | tf_op jit(solution)/shard_map/while/body/eval_jaxpr/cond
  1080.4 6.6 collective-permute-start.1
  1081.7 5.3 collective-permute-start
  1097.0 28.6 %slice-start.2 = ((s8[8388608]{0:T(1024)(128)(4,1)}), s8[4194304]{0:T(1024)(128)(4,1)S(1)}, s32[]{:S(2)}) async-start(s8[8388608]{0:T(1024)(128)(4,1)} %bitcast.44), calls=%async_computation.4 | async-start | bytes 8388608 | tf_op jit(solution)/shard_map/while/body/eval_jaxpr/cond
  1128.4 12.6 collective-permute-start.1
  1129.7 11.3 collective-permute-start
  1151.0 28.6 %slice-start.2 = ((s8[8388608]{0:T(1024)(128)(4,1)}), s8[4194304]{0:T(1024)(128)(4,1)S(1)}, s32[]{:S(2)}) async-start(s8[8388608]{0:T(1024)(128)(4,1)} %bitcast.44), calls=%async_computation.4 | async-start | bytes 8388608 | tf_op jit(solution)/shard_map/while/body/eval_jaxpr/cond
  1182.3 6.6 collective-permute-start.1
  1183.6 5.3 collective-permute-start
  1242.2 404.4 %copy-start = (f32[1,1,131072]{2,1,0:T(1,128)S(1)}, f32[1,1,131072]{2,1,0:T(1,128)}, u32[]{:S(2)}) copy-start(f32[1,1,131072]{2,1,0:T(1,128)} %param.16) | copy-start | bytes 1572868
  1242.2 404.4 %copy-start.1 = (f32[1,1,131072]{2,1,0:T(1,128)S(1)}, f32[1,1,131072]{2,1,0:T(1,128)}, u32[]{:S(2)}) copy-start(f32[1,1,131072]{2,1,0:T(1,128)} %param.17) | copy-start | bytes 1572868
  1242.2 404.4 %copy-start.2 = (f32[1,1,131072]{2,1,0:T(1,128)S(1)}, f32[1,1,131072]{2,1,0:T(1,128)}, u32[]{:S(2)}) copy-start(f32[1,1,131072]{2,1,0:T(1,128)} %param.18) | copy-start | bytes 1572868
  1242.2 567.9 %all-gather.2.cloned.1.call-start = ((), (), s32[]{:S(2)}) async-start(), calls=%async_computation | async-start | bytes 34078720 | tf_op jit(solution)/shard_map/all_gather | solution.py:145
  (42 other events, 316.5 us)
Sparse Core Ops, SparseCore 0:
  1242.3 337.6 all-reduce.3
  1652.6 157.4 all-gather.1
where the time goes:
time: 1860 us
  matrix products  734 us (39%)
  waiting for transfers between devices  493 us (27%)
  local copies, waits for them, and re-layouts  316 us (17%)
  starting transfers between devices  120 us (6%)
  other arithmetic  95.9 us (5%)
  blocking collectives  63.1 us (3%)
    unnamed x3, waiting for transfers between devices  336 us
    dot_general x16, matrix products, stage_backward(): jnp.einsum('nk,nf->kf', saved_in[layer_idx], grad_pre, preferred_element_...  233 us
    dot_general x16, matrix products, stage_backward(): jnp.einsum('nf,nk->fk', act_bf, grad_h, preferred_element_type=jnp.float32)  225 us
    slice x1, local copies, waits for them, and re-layouts, split_layer(): w_flat[half_len:].reshape(4 * d_model, d_model)  184 us
    all_gather x1, waiting for transfers between devices, device_step(): lax.all_gather(w_new.astype(jnp.bfloat16), 'data', axis=2, tiled=True)  157 us
    dot_general x16, matrix products, stage_backward(): jnp.einsum('nk,fk->nf', grad_h, w_out_list[layer_idx], preferred_element_...  96.6 us
    ppermute x18, starting transfers between devices, tick_body(): recv_act = lax.ppermute(act_out, 'stage', fwd_pairs)  96.4 us
    dot_general x16, matrix products, stage_forward(): jnp.dot(hidden, w_in, preferred_element_type=jnp.float32)  94.3 us
  transfers between devices with their start and end apart: 38, of which 2 were waited for; matrix products, arithmetic and copies ran while one was open for 2% of the time, Pallas kernels for 0%

commit v1 on v0

v1 whole, which is shorter than its diff:
```python
import functools
import math
import jax
import jax.numpy as jnp
from jax import lax
from jax.experimental import pallas as pl
from jax.experimental.pallas import tpu as pltpu
from jax.sharding import PartitionSpec as P

ADAM_BETA1 = 0.9
ADAM_BETA2 = 0.95
ADAM_EPS = 1e-8
WEIGHT_DECAY = 0.1
ADAM_STEP = 10
LR_BASE = 0.05
MESH = pl.DeviceIdType.MESH
MIB = 1024 * 1024

SUBS = 4
SUB_ROWS = 256
ALL = slice(None)
RS_ORDER = ((2, 1, 0), (1, 0, 2), (0, 2, 1))
AG_ORDER = ((0, 1, 2), (1, 2, 0), (2, 0, 1))


def rs_split():
    table = {}
    for s in range(SUBS):
        sizes = [11, 11, 11]
        sizes[(s + 2) % 3] = 10
        start = 32 * s
        for c in range(3):
            n = sizes[c]
            first = (n + (s + c) % 2) // 2
            table[s, c] = (start * 8, first * 8, (n - first) * 8)
            start += n
    return table


def coords_of(me):
    return [me // 16, lax.rem(me // 4, 4), lax.rem(me, 4)]


def peer(coords, pos, delta):
    moved = list(coords)
    moved[pos] = lax.rem(coords[pos] + (delta + 4), 4)
    return moved[0] * 16 + moved[1] * 4 + moved[2]


def greet(coords):
    barrier = pltpu.get_barrier_semaphore()
    for pos in range(3):
        for delta in (1, -1):
            pl.semaphore_signal(barrier, inc=1, device_id={"data": peer(coords, pos, delta)}, device_id_type=MESH)
    pl.semaphore_wait(barrier, 6)


def rs_kernel(g_ref, out_ref, ra1, rb1, lb, own, ra2, rb2, ra3, rb3, ssem, rsem, lsem):
    coords = coords_of(lax.axis_index("data"))
    table = rs_split()
    ra = (ra1, ra2, ra3)
    rb = (rb1, rb2, rb3)
    copies = {}
    deltas = (1, -1)

    def rows(s, c, half):
        start, n0, n1 = table[s, c]
        if half == 0:
            return 0, n0
        if half == 1:
            return n0, n1
        return 0, n0 + n1

    def lead(ph, c, k):
        order = RS_ORDER[c]
        left = [p for p in (0, 1, 2) if p != order[0]]
        idx = []
        for p in left:
            if ph == 1:
                idx.append(k if p == order[1] else pl.ds(0, 4))
            else:
                idx.append(coords[order[1]] if p == order[1] else k)
        return tuple(idx)

    def lead_t(ph, c, k, t):
        if ph == 0:
            return (t // 4, lax.rem(t, 4))
        return tuple(t if not isinstance(i, jax.Array) and isinstance(i, pl.Slice) else i for i in lead(ph, c, k))

    def source(ph, s, c, k, half):
        lo, n = rows(s, c, half)
        if ph == 0:
            idx = [pl.ds(0, 4)] * 3
            idx[RS_ORDER[c][0]] = k
            return g_ref.at[tuple(idx) + (pl.ds(table[s, c][0] + lo, n), ALL)]
        return own.at[(s * 3 + c,) + lead(ph, c, k) + (pl.ds(lo, n), ALL)]

    def slot(ref, ph, i, lo, n):
        return ref.at[(i,) + (pl.ds(0, 4),) * (2 - ph) + (pl.ds(lo, n), ALL)]

    def start(ph, s, c, d, piece, src, dst):
        i = (((ph * SUBS + s) * 3 + c) * 2 + d) * 3 + piece
        target = peer(coords, RS_ORDER[c][ph], deltas[d])
        copy = pltpu.make_async_remote_copy(src_ref=src, dst_ref=dst, send_sem=ssem.at[i], recv_sem=rsem.at[i],
                                            device_id={"data": target}, device_id_type=MESH)
        copy.start()
        copies[ph, s, c, d, piece] = copy

    def at(c, ph, delta):
        return lax.rem(coords[RS_ORDER[c][ph]] + (delta + 4), 4)

    def send_a(ph, s, c):
        for d in range(2):
            n = rows(s, c, d)[1]
            start(ph, s, c, d, 0, source(ph, s, c, at(c, ph, 2), d), slot(ra[ph], ph, s * 6 + c * 2 + d, 0, n))

    def send_b1(ph, s, c):
        for d in range(2):
            lo, n = rows(s, c, 1 - d)
            start(ph, s, c, d, 1, source(ph, s, c, at(c, ph, deltas[d]), 1 - d), slot(rb[ph], ph, s * 6 + c * 2 + d, lo, n))

    def load(s, c):
        for d in range(2):
            i = s * 9 + c * 3 + d
            n = rows(s, c, d)[1]
            copy = pltpu.make_async_copy(source(0, s, c, at(c, 0, deltas[d]), d), slot(lb, 0, s * 6 + c * 2 + d, 0, n), lsem.at[i])
            copy.start()
            copies["lb", s, c, d] = copy
        n = rows(s, c, 2)[1]
        copy = pltpu.make_async_copy(source(0, s, c, at(c, 0, 0), 2), slot(own, 0, s * 3 + c, 0, n), lsem.at[s * 9 + c * 3 + 2])
        copy.start()
        copies["own", s, c] = copy

    def forward(ph, s, c):
        for d in range(2):
            i = s * 6 + c * 2 + d
            lo, n = rows(s, c, d)
            if ph == 0:
                copies["lb", s, c, d].wait()
            copies[ph, s, c, d, 0].wait_recv()
            buf = ra[ph]
            k = at(c, ph, deltas[d])
            if ph == 2:
                buf[i, pl.ds(0, n), :] += own[(s * 3 + c,) + lead(2, c, k) + (pl.ds(lo, n), ALL)]
            elif ph == 1:
                def body1(t, carry, i=i, n=n, lo=lo, buf=buf, k=k):
                    buf[i, t, pl.ds(0, n), :] += own[(s * 3 + c,) + lead_t(1, c, k, t) + (pl.ds(lo, n), ALL)]
                    return carry
                lax.fori_loop(0, 4, body1, 0)
            else:
                def body0(t, carry, i=i, n=n, buf=buf):
                    u, v = t // 4, lax.rem(t, 4)
                    buf[i, u, v, pl.ds(0, n), :] += lb[i, u, v, pl.ds(0, n), :]
                    return carry
                lax.fori_loop(0, 16, body0, 0)
            start(ph, s, c, d, 2, slot(buf, ph, i, 0, n), slot(rb[ph], ph, i, lo, n))

    def finish(ph, s, c):
        if ph == 0:
            copies["own", s, c].wait()
        for d in range(2):
            copies[ph, s, c, d, 1].wait_recv()
            copies[ph, s, c, d, 2].wait_recv()
        n = rows(s, c, 2)[1]
        i, j = s * 6 + c * 2, s * 3 + c
        buf = rb[ph]
        k = at(c, ph, 0)
        span = pl.ds(0, n)
        if ph == 2:
            total = own[(j,) + lead(2, c, k) + (span, ALL)] + buf[i, span, :] + buf[i + 1, span, :]
            out_ref[pl.ds(table[s, c][0], n), :] = total
            return
        if ph == 1:
            def body1(t, carry):
                where = (j,) + lead_t(1, c, k, t) + (span, ALL)
                own[where] = own[where] + buf[i, t, span, :] + buf[i + 1, t, span, :]
                return carry
            lax.fori_loop(0, 4, body1, 0)
            return

        def body0(t, carry):
            u, v = t // 4, lax.rem(t, 4)
            own[j, u, v, span, :] = own[j, u, v, span, :] + buf[i, u, v, span, :] + buf[i + 1, u, v, span, :]
            return carry
        lax.fori_loop(0, 16, body0, 0)

    def st0(s):
        for c in range(3):
            send_a(0, s, c)
            load(s, c)

    def st0b(s):
        for c in range(3):
            send_b1(0, s, c)

    def mid(ph, s):
        for c in range(3):
            forward(ph, s, c)

    def turn(ph, s):
        for c in range(3):
            finish(ph, s, c)
            if ph < 2:
                send_a(ph + 1, s, c)
                send_b1(ph + 1, s, c)

    def opening(s):
        if s < SUBS:
            st0(s)

    def second(s):
        if s < SUBS:
            st0b(s)

    steps = []
    for s in range(SUBS):
        done = 3 * s + 4
        steps.append((max(s, 3 * s - 1), 0, mid, 0, s))
        for ph in range(3):
            steps.append((done + 4 * ph, 1, turn, ph, s))
            if ph:
                steps.append((done + 4 * ph - 2, 1, mid, ph, s))
    greet(coords)
    opening(0)
    opening(1)
    second(0)
    for _, _, act, ph, s in sorted(steps, key=lambda e: e[:2]):
        act(ph, s)
        if act is mid and ph == 0:
            opening(s + 2)
            second(s + 1)
    for key, copy in copies.items():
        if not isinstance(key[0], str):
            copy.wait_send()


def reduce_scatter(g):
    sems = 3 * SUBS * 3 * 2 * 3
    f32 = jnp.float32
    return pl.pallas_call(
        rs_kernel,
        out_shape=jax.ShapeDtypeStruct((1024, 128), f32),
        in_specs=[pl.BlockSpec(memory_space=pl.ANY)],
        out_specs=pl.BlockSpec(memory_space=pltpu.VMEM),
        scratch_shapes=[
            pltpu.VMEM((SUBS * 6, 4, 4, 48, 128), f32),
            pltpu.VMEM((SUBS * 6, 4, 4, 88, 128), f32),
            pltpu.VMEM((SUBS * 6, 4, 4, 48, 128), f32),
            pltpu.VMEM((SUBS * 3, 4, 4, 88, 128), f32),
            pltpu.VMEM((SUBS * 6, 4, 48, 128), f32),
            pltpu.VMEM((SUBS * 6, 4, 88, 128), f32),
            pltpu.VMEM((SUBS * 6, 48, 128), f32),
            pltpu.VMEM((SUBS * 6, 88, 128), f32),
            pltpu.SemaphoreType.DMA((sems,)),
            pltpu.SemaphoreType.DMA((sems,)),
            pltpu.SemaphoreType.DMA((SUBS * 9,)),
        ],
        compiler_params=pltpu.CompilerParams(collective_id=0, has_side_effects=True, vmem_limit_bytes=60 * MIB),
        name="grad_rs",
    )(g)


def ag_split():
    table = []
    start = 0
    for c, n in enumerate((22, 21, 21)):
        first = (n + c % 2) // 2
        table.append((start * 16, first * 16, (n - first) * 16))
        start += n
    return table


def ag_kernel(w_ref, out_ref, ssem, rsem, lsem):
    coords = coords_of(lax.axis_index("data"))
    table = ag_split()
    deltas = (1, -1)
    copies = {}

    def rows(c, half):
        start, n0, n1 = table[c]
        return (start, n0) if half == 0 else (start + n0, n1)

    def region(c, unit, shift, half):
        first, second, third = AG_ORDER[c]
        idx = [None] * 3
        if unit == 0:
            idx[first], idx[second], idx[third] = lax.rem(coords[first] + (shift + 4), 4), coords[second], coords[third]
        elif unit == 1:
            idx[first], idx[second], idx[third] = pl.ds(0, 4), lax.rem(coords[second] + (shift + 4), 4), coords[third]
        else:
            q = lax.rem(coords[second] + ((0, -1, 1, 2)[unit - 2] + 4), 4)
            idx[first], idx[second], idx[third] = pl.ds(0, 4), q, lax.rem(coords[third] + (shift + 4), 4)
        lo, n = rows(c, half)
        return out_ref.at[tuple(idx) + (pl.ds(lo, n), ALL)]

    def start(c, unit, d, piece, src, dst):
        i = ((unit * 3 + c) * 2 + d) * 3 + piece
        target = peer(coords, AG_ORDER[c][min(unit, 2)], deltas[d])
        copy = pltpu.make_async_remote_copy(src_ref=src, dst_ref=dst, send_sem=ssem.at[i], recv_sem=rsem.at[i],
                                            device_id={"data": target}, device_id_type=MESH)
        copy.start()
        copies[c, unit, d, piece] = copy

    def begin(unit):
        for c in range(3):
            for d in range(2):
                for piece, half in ((0, d), (1, 1 - d)):
                    lo, n = rows(c, half)
                    here = region(c, unit, 0, half)
                    src = w_ref.at[pl.ds(lo, n), :] if unit == 0 else here
                    start(c, unit, d, piece, src, here)

    def middle(unit):
        for c in range(3):
            for d in range(2):
                copies[c, unit, d, 0].wait_recv()
                part = region(c, unit, -deltas[d], d)
                start(c, unit, d, 2, part, part)

    def arrive(unit, piece):
        for c in range(3):
            for d in range(2):
                copies[c, unit, d, piece].wait_recv()

    greet(coords)
    local = pltpu.make_async_copy(w_ref, out_ref.at[coords[0], coords[1], coords[2]], lsem)
    local.start()
    begin(0)
    middle(0)
    arrive(0, 1)
    arrive(0, 2)
    local.wait()
    begin(1)
    begin(2)
    middle(1)
    arrive(1, 1)
    begin(3)
    begin(4)
    middle(2)
    arrive(1, 2)
    begin(5)
    middle(3)
    middle(4)
    middle(5)
    for unit in (2, 3, 4, 5):
        arrive(unit, 1)
        arrive(unit, 2)
    for copy in copies.values():
        copy.wait_send()


def all_gather_rows(w):
    sems = 6 * 3 * 2 * 3
    return pl.pallas_call(
        ag_kernel,
        out_shape=jax.ShapeDtypeStruct((4, 4, 4, 1024, 128), w.dtype),
        in_specs=[pl.BlockSpec(memory_space=pltpu.VMEM)],
        out_specs=pl.BlockSpec(memory_space=pl.ANY),
        scratch_shapes=[
            pltpu.SemaphoreType.DMA((sems,)),
            pltpu.SemaphoreType.DMA((sems,)),
            pltpu.SemaphoreType.DMA,
        ],
        compiler_params=pltpu.CompilerParams(collective_id=1, has_side_effects=True),
        name="weight_ag",
    )(w)


def wgrad_kernel(x_ref, du_ref, a_ref, g_ref, out_ref):
    part = pl.program_id(1)

    @pl.when(part == 0)
    def _():
        def body(m, carry):
            cols = pl.ds(pl.multiple_of(m * 256, 256), 256)
            val = lax.dot_general(x_ref[:, cols], du_ref[...], (((0,), (0,)), ((), ())), preferred_element_type=jnp.float32)
            for ct in range(8):
                out_ref[pl.ds(m * 8, 8), ct * 32:(ct + 1) * 32, :] = val[:, ct * 128:(ct + 1) * 128].reshape(8, 32, 128)
            return carry
        lax.fori_loop(0, 4, body, 0)

    @pl.when(part == 1)
    def _():
        def body(m, carry):
            cols = pl.ds(pl.multiple_of(m * 1024, 1024), 1024)
            val = lax.dot_general(a_ref[:, cols], g_ref[...], (((0,), (0,)), ((), ())), preferred_element_type=jnp.float32)
            for ct in range(2):
                out_ref[pl.ds(m * 8, 8), ct * 128:(ct + 1) * 128, :] = val[:, ct * 128:(ct + 1) * 128].reshape(8, 128, 128)
            return carry
        lax.fori_loop(0, 4, body, 0)


def weight_grads(x, du, a, g):
    rows, d = x.shape
    return pl.pallas_call(
        wgrad_kernel,
        grid=(SUBS, 2),
        out_shape=jax.ShapeDtypeStruct((64, 1024, 128), jnp.float32),
        in_specs=[
            pl.BlockSpec((rows, d), lambda s, p: (0, 0)),
            pl.BlockSpec((rows, d), lambda s, p: (0, s)),
            pl.BlockSpec((rows, 4 * d), lambda s, p: (0, 0)),
            pl.BlockSpec((rows, d // 4), lambda s, p: (0, s)),
        ],
        out_specs=pl.BlockSpec((32, SUB_ROWS, 128), lambda s, p: (p, s, 0)),
        compiler_params=pltpu.CompilerParams(vmem_limit_bytes=56 * MIB, dimension_semantics=("arbitrary", "arbitrary")),
        cost_estimate=pl.CostEstimate(flops=4 * rows * d * 4 * d, bytes_accessed=52 * MIB, transcendentals=0),
        name="wgrad",
    )(x, du, a, g)


def unflatten_kernel(cols, w_ref, o_ref, wide):
    n = wide.shape[0] // 8
    for j in range(n):
        wide[j * 8:(j + 1) * 8, :] = w_ref[:, j * 1024:(j + 1) * 1024].astype(jnp.float32).reshape(8, 128)
    blocks = cols // 128
    rows = o_ref.shape[0]
    for cb in range(blocks):
        o_ref[:, cb * 128:(cb + 1) * 128] = wide[pl.ds(cb, rows, stride=blocks), :].astype(o_ref.dtype)


def unflatten(flat, part, cols):
    chunk = 131072
    steps = flat.shape[1] // 2 // chunk
    rows = chunk // cols
    return pl.pallas_call(
        functools.partial(unflatten_kernel, cols),
        grid=(steps,),
        out_shape=jax.ShapeDtypeStruct((rows * steps, cols), flat.dtype),
        in_specs=[pl.BlockSpec((1, chunk), lambda i: (0, part * steps + i))],
        out_specs=pl.BlockSpec((rows, cols), lambda i: (i, 0)),
        scratch_shapes=[pltpu.VMEM((chunk // 128, 128), jnp.float32)],
        name="unflatten",
    )(flat)


def flatten_kernel(w_ref, o_ref):
    for j in range(o_ref.shape[1] // 2048):
        o_ref[:, j * 2048:(j + 1) * 2048] = w_ref[j * 16:(j + 1) * 16, :].astype(jnp.float32).reshape(1, 2048).astype(o_ref.dtype)


def flatten(rows):
    chunk = 131072
    total = rows.size
    return pl.pallas_call(
        flatten_kernel,
        grid=(total // chunk,),
        out_shape=jax.ShapeDtypeStruct((1, total), rows.dtype),
        in_specs=[pl.BlockSpec((chunk // 128, 128), lambda i: (i, 0))],
        out_specs=pl.BlockSpec((1, chunk), lambda i: (0, i)),
        name="flatten",
    )(rows)


def gelu_tanh(z_val):
    return jax.nn.gelu(z_val, approximate=True)


def dot32(a, b, dims=((1,), (0,))):
    return lax.dot_general(a, b, (dims, ((), ())), preferred_element_type=jnp.float32)


def block_forward(x, w1, w2):
    u = dot32(x, w1).astype(jnp.bfloat16)
    a = gelu_tanh(u.astype(jnp.float32)).astype(jnp.bfloat16)
    return u, a, (x.astype(jnp.float32) + dot32(a, w2)).astype(jnp.bfloat16)


def pre_grad(u, g, w2):
    e = dot32(g, w2, ((1,), (1,)))
    _, pull = jax.vjp(gelu_tanh, u.astype(jnp.float32))
    return pull(e)[0].astype(jnp.bfloat16)


def adam_update(w_master, m_prior, v_prior, grad_part, clip_scale, d_model):
    scaled = clip_scale * grad_part
    m_new = ADAM_BETA1 * m_prior + (1.0 - ADAM_BETA1) * scaled
    v_new = ADAM_BETA2 * v_prior + (1.0 - ADAM_BETA2) * scaled * scaled
    m_hat = m_new / (1.0 - ADAM_BETA1 ** ADAM_STEP)
    v_hat = v_new / (1.0 - ADAM_BETA2 ** ADAM_STEP)
    learn_rate = LR_BASE / math.sqrt(d_model)
    w_new = w_master - learn_rate * (m_hat / (jnp.sqrt(v_hat) + ADAM_EPS) + WEIGHT_DECAY * w_master)
    return w_new, m_new, v_new


def solution(mesh):
    data_size = mesh.shape['data']

    def device_step(x_in, targets, w_work, w_master, m_prior, v_prior, clip_tau):
        d = x_in.shape[-1]
        rows = x_in.shape[0] * x_in.shape[1]
        token_count = rows * data_size
        x0 = x_in.reshape(rows, d)
        t0 = targets.reshape(rows, d)
        flat = w_work.reshape(1, -1)
        w1 = unflatten(flat, 0, 4 * d)
        w2 = unflatten(flat, 1, d)
        stage = lax.axis_index('stage')
        is_first = stage == 0
        bf = jnp.bfloat16
        wide = jnp.zeros((rows, 4 * d), bf)
        narrow = jnp.zeros((rows, d), bf)

        u0, a0, h0 = lax.cond(is_first, lambda: block_forward(x0, w1, w2), lambda: (wide, wide, narrow))
        h_recv = lax.ppermute(h0, 'stage', [(0, 1)])

        def last_stage():
            u, a, y = block_forward(h_recv, w1, w2)
            res = y.astype(jnp.float32) - t0.astype(jnp.float32)
            loss = 0.5 * jnp.sum(res * res)
            g = (res / token_count).astype(bf)
            du = pre_grad(u, g, w2)
            g_in = (g.astype(jnp.float32) + dot32(du, w1, ((1,), (1,)))).astype(bf)
            return h_recv, u, a, g, du, g_in, loss

        x, u, a, g1, du1, g_in, loss_acc = lax.cond(
            is_first, lambda: (x0, u0, a0, narrow, wide, narrow, jnp.zeros((), jnp.float32)), last_stage)
        g_recv = lax.ppermute(g_in, 'stage', [(1, 0)])
        g, du = lax.cond(is_first, lambda: (g_recv, pre_grad(u, g_recv, w2)), lambda: (g1, du1))

        grads = weight_grads(x, du, a, g)
        part = reduce_scatter(grads.reshape(4, 4, 4, 1024, 128))
        totals = lax.psum(jnp.stack([jnp.sum(part * part), loss_acc]), ('stage', 'data'))
        clip_scale = jnp.minimum(1.0, clip_tau / jnp.sqrt(totals[0]))
        early = lax.axis_index('data') < data_size // 2
        part_flat = jnp.where(early, part.reshape(32, 32, 128).transpose(1, 0, 2).reshape(1, 1, -1),
                              part.reshape(8, 128, 128).transpose(1, 0, 2).reshape(1, 1, -1))
        w_new, m_new, v_new = adam_update(w_master, m_prior, v_prior, part_flat, clip_scale, d)
        gathered = all_gather_rows(w_new.astype(bf).reshape(1024, 128))
        return totals[1] / token_count, flatten(gathered.reshape(-1, 128)).reshape(1, 1, -1), w_new, m_new, v_new

    row_spec = P(None, 'data', None)
    shard_spec = P('stage', None, 'data')
    stage_spec = P('stage', None, None)
    return jax.shard_map(device_step, mesh=mesh, in_specs=(row_spec, row_spec, stage_spec, shard_spec, shard_spec, shard_spec, P()), out_specs=(P(), stage_spec, shard_spec, shard_spec, shard_spec), check_vma=False)
```

time: 1860 us -> 554 us (0.30)
  matrix products: 734 us -> 52 us
  waiting for transfers between devices: 493 us -> 57.8 us
  Pallas kernels: 0 us -> 325 us
  local copies, waits for them, and re-layouts: 316 us -> 15.3 us
  starting transfers between devices: 120 us -> 3.91 us
  other arithmetic: 95.9 us -> 14.1 us
    dot_general x96 -> x3, matrix products: 734 us -> 52 us  [dot32(): lax.dot_general(a, b, (dims, ((), ())), preferred_element_type=jnp.float32)]
    unnamed x3 -> x0, waiting for transfers between devices: 336 us -> none
    pallas_call x0 -> x6, Pallas kernels: none -> 325 us  [the longest x1 123 us: reduce_scatter(): pl.pallas_call(rs_kernel, out_shape=jax.ShapeDtypeStruct((1024, 128), f32...]
    slice x1, local copies, waits for them, and re-layouts: 184 us -> 0.61 us  [device_step(): clip_scale = jnp.minimum(1.0, clip_tau / jnp.sqrt(totals[0]))]
    all_gather x1 -> x0, waiting for transfers between devices: 157 us -> none  [device_step(): lax.all_gather(w_new.astype(jnp.bfloat16), 'data', axis=2, tiled=True)]
    ppermute x36 -> x2, starting transfers between devices: 120 us -> 3.91 us  [the longest x1 2.63 us: device_step(): h_recv = lax.ppermute(h0, 'stage', [(0, 1)])]
    unnamed x12 -> x8, local copies, waits for them, and re-layouts: 66.8 us -> 1.32 us
    ppermute x36 -> x2, waiting for transfers between devices: 0.09 us -> 57.8 us  [the longest x1 55.4 us: device_step(): g_recv = lax.ppermute(g_in, 'stage', [(1, 0)])]
  transfers between devices with their start and end apart: 38 -> 2, of which waited for: 2 -> 2; matrix products, arithmetic and copies ran while one was open for 2% -> 0% of each run, Pallas kernels for 0% -> 0%
where the time goes in v1:
time: 554 us; the launch traced here: 544 us
  Pallas kernels  325 us (59%)
  blocking collectives  63.2 us (11%)
  waiting for transfers between devices  57.8 us (10%)
  matrix products  52 us (9%)
  local copies, waits for them, and re-layouts  15.3 us (3%)
  other arithmetic  14.1 us (3%)
  loops' own time  8.48 us (2%)
    pallas_call x1, Pallas kernels, reduce_scatter(): pl.pallas_call(rs_kernel, out_shape=jax.ShapeDtypeStruct((1024, 128), f32...  123 us
    pallas_call x1, Pallas kernels, all_gather_rows(): pl.pallas_call(ag_kernel, out_shape=jax.ShapeDtypeStruct((4, 4, 4, 1024,...  69.4 us
    psum x1, blocking collectives, device_step(): lax.psum(jnp.stack([jnp.sum(part * part), loss_acc]), ('stage', 'data'))  63.2 us
    ppermute x1, waiting for transfers between devices, device_step(): g_recv = lax.ppermute(g_in, 'stage', [(1, 0)])  55.4 us
    dot_general x3, matrix products, dot32(): lax.dot_general(a, b, (dims, ((), ())), preferred_element_type=jnp.float32)  52 us
    pallas_call x1, Pallas kernels, flatten(): pl.pallas_call(flatten_kernel, grid=(total // chunk,), out_shape=jax.Shap...  51.1 us
    pallas_call x2, Pallas kernels, unflatten(): pl.pallas_call(functools.partial(unflatten_kernel, cols), grid=(steps,),...  49.6 us
    pallas_call x1, Pallas kernels, weight_grads(): pl.pallas_call(wgrad_kernel, grid=(SUBS, 2), out_shape=jax.ShapeDtypeStru...  32.2 us
  transfers between devices with their start and end apart: 2, of which 2 were waited for; matrix products, arithmetic and copies ran while one was open for 0% of the time, Pallas kernels for 0%

profile of v1, /device:TPU:0, one launch (start us, length us, event | category | flops | bytes accessed | tf_op | source)
XLA Modules:
  0.0 544.1 jit_solution(5198642422162058856)
XLA Ops:
  0.6 23.2 %unflatten.3 = bf16[4096,1024]{1,0:T(8,128)(2,1)} custom-call(bf16[1,8388608]{1,0:T(2,128)(2,1)} %bitcast.36), custom_call_target="tpu_custom_call" | custom-call | tf_op jit(solution)/shard_map/unflatten/pallas_call | solution.py:426
  23.8 26.4 %unflatten.2 = bf16[1024,4096]{1,0:T(8,128)(2,1)} custom-call(bf16[1,8388608]{1,0:T(2,128)(2,1)} %bitcast.37), custom_call_target="tpu_custom_call" | custom-call | tf_op jit(solution)/shard_map/unflatten/pallas_call | solution.py:426
  50.2 29.5 %conditional.3 = (bf16[1024,4096]{1,0:T(8,128)(2,1)}, bf16[1024,4096]{1,0:T(8,128)(2,1)}, bf16[1024,1024]{1,0:T(8,128)(2,1)S(1)}) conditional(s32[]{:T(128)} %convert_element_type.66, () %tuple.33, (bf16[1024,1024]{1,0:T(8,128)(2,1)}, bf16[1024,4096]{1,0:T(8,128)(2,1)}, bf16[4096,1024]{1,0:T(8,128)(2,1)}) %tuple.55), branch_computations={%region_0.0_spmd, %region_1.0_spmd} | conditional | flops 17229152256 | bytes 90177616 | solution.py:504
  50.2 0.0 copy-start
  50.2 0.0 copy-start.2
  50.2 18.0 %fusion.5 = (bf16[1024,4096]{1,0:T(8,128)(2,1)}, bf16[1024,4096]{1,0:T(8,128)(2,1)}) fusion(bf16[1024,1024]{1,0:T(8,128)(2,1)} %get-tuple-element.32, bf16[1024,4096]{1,0:T(8,128)(2,1)} %get-tuple-element.33), kind=kOutput, calls=%fused_computation.9 | convolution fusion | flops 8636071936 | bytes 27262976 | tf_op jit(solution)/shard_map/cond/branch_1_fun/dot_general | solution.py:460
  68.2 0.0 copy-done
  68.2 0.0 copy-done.2
  68.3 11.4 %add_convert_fusion = bf16[1024,1024]{1,0:T(8,128)(2,1)S(1)} fusion(bf16[1024,1024]{1,0:T(8,128)(2,1)S(1)} %copy-done.2, bf16[1024,4096]{1,0:T(8,128)(2,1)} %get-tuple-element.92, bf16[4096,1024]{1,0:T(8,128)(2,1)S(1)} %copy-done), kind=kOutput, calls=%fused_computation.11 | convolution fusion | flops 8593080320 | bytes 20971520 | tf_op jit(solution)/shard_map/cond/branch_1_fun/dot_general | solution.py:460
  79.7 2.6 collective-permute-start
  82.3 2.4 collective-permute-done
  84.8 17.7 %conditional.4 = (bf16[1024,1024]{1,0:T(8,128)(2,1)}, bf16[1024,4096]{1,0:T(8,128)(2,1)}, bf16[1024,4096]{1,0:T(8,128)(2,1)}, bf16[1024,1024]{1,0:T(8,128)(2,1)}...) conditional(s32[]{:T(128)} %convert_element_type.66, (bf16[1024,1024]{1,0:T(8,128)(2,1)}, ...), branch_computations={%region_2.0_spmd, %region_4.0_spmd} | conditional | flops 34507587584 | bytes 140509312 | solution.py:516
  93.2 3.1 copy.28
  96.3 4.3 broadcast_in_dim.11
  100.6 1.6 broadcast_in_dim.10
  102.2 0.3 broadcast_in_dim.10.clone
  102.5 0.0 copy-start.7
  102.5 1.3 copy-done.7
  103.8 1.3 collective-permute-start.1
  105.8 55.4 %collective-permute-done.1 = bf16[1024,1024]{1,0:T(8,128)(2,1)S(1)} collective-permute-done((bf16[1024,1024]{1,0:T(8,128)(2,1)}, bf16[1024,1024]{1,0:T(8,128)(2,1)S(1)}, u32[]{:S(2)}, u32[]{:S(2)}) %collective-permute-start.1) | collective-permute-done | bytes 2097184 | tf_op jit(solution)/shard_map/ppermute | solution.py:518
  161.2 23.9 %conditional.5 = ((bf16[1024,1024]{1,0:T(8,128)(2,1)}, bf16[1024,4096]{1,0:T(8,128)(2,1)})) conditional(s32[]{:T(128)} %convert_element_type.66, (bf16[1024,1024]{1,0:T(8,128)(2,1)}, bf16[1024,4096]{1,0:T(8,128)(2,1)}) %tuple.37, (bf16[1024,1024]{1,0:T(8,128)(2,1)S(1)}, bf16[4096,1024]{1,0:T(8,128)(2,1)}, bf16[1024,4096]{1,0:T(8,128)(2,1)}) %tuple.38), branch_computations={%region_5.0_spmd, %region_6.0_spmd} | conditional | flops 8678014976 | bytes 31457304 | solution.py:519
  161.2 22.6 %fusion.19 = bf16[1024,4096]{1,0:T(8,128)(2,1)} fusion(bf16[1024,4096]{1,0:T(8,128)(2,1)} %get-tuple-element.44, bf16[1024,1024]{1,0:T(8,128)(2,1)S(1)} %get-tuple-element.110, bf16[4096,1024]{1,0:T(8,128)(2,1)} %get-tuple-element.43), kind=kOutput, calls=%fused_computation.40 | convolution fusion | flops 8678014976 | bytes 27262976 | tf_op jit(solution)/shard_map/cond/branch_1_fun/dot_general | solution.py:460
  183.7 1.4 copy.37
  185.1 32.2 %wgrad.1 = f32[64,1024,128]{2,1,0:T(8,128)} custom-call(bf16[1024,1024]{1,0:T(8,128)(2,1)} %get-tuple-element.65.x_ref, bf16[1024,4096]{1,0:T(8,128)(2,1)} %get-tuple-element.70.du_ref, bf16[1024,4096]{1,0:T(8,128)(2,1)} %get-tuple-element.71.a_ref, bf16[1024,1024]{1,0:T(8,128)(2,1)} %get-tuple-element.72.g_ref), custom_call_target="tpu_custom_call" | custom-call | flops 17179869184 | bytes 54525952 | tf_op jit(solution)/shard_map/wgrad/pallas_call | solution.py:395
  217.3 0.0 copy-start.3
  217.3 0.0 copy-start.4
  217.3 0.0 copy-start.5
  217.3 122.7 %grad_rs.1 = f32[1024,128]{1,0:T(8,128)} custom-call(f32[4,4,4,1024,128]{4,3,2,1,0:T(8,128)} %bitcast.40), custom_call_target="tpu_custom_call" | custom-call | tf_op jit(solution)/shard_map/grad_rs/pallas_call | solution.py:240
  340.0 1.8 multiply_reduce_fusion.1
  341.8 1.3 copy.13
  343.1 0.7 pad_maximum_fusion
  343.8 1.3 copy.14
  345.2 63.2 %psum.7 = f32[2]{0:T(128)S(1)} all-reduce(f32[2]{0:T(128)S(1)} %pad_maximum_fusion), channel_id=1, replica_groups=mesh['stage'=2,'data'=64] {'stage','data'}, use_global_device_ids=true, to_apply=%region_8.0 | all-reduce | flops 2 | bytes 16 | tf_op jit(solution)/shard_map/psum | solution.py:523
  408.4 0.6 fusion.28
  409.7 0.0 copy-done.3
  409.7 0.0 copy-done.4
  409.7 0.0 copy-done.5
  409.7 11.6 %convert_reduce_fusion = (bf16[131072]{0:T(1024)(128)(2,1)}, f32[1,1,131072]{2,1,0:T(1,128)}, f32[1,1,131072]{2,1,0:T(1,128)}, f32[1,1,131072]{2,1,0:T(1,128)}) fusion(f32[1,1,131072]{2,1,0:T(1,128)S(1)} %copy-done.3, f32[1,1,131072]{2,1,0:T(1,128)S(1)} %bitcast.43, f32[1,1,131072]{2,1,0:T(1,128)S(1)} %bitcast.44, pred[]{:T(512)S(6)} %lt.3, f32[]{:T(128)S(6)} %min.3, ...), kind=kLoop, calls=%fused_computation.50 | loop fusion | flops 2359296 | bytes 4456453 | tf_op jit(solution)/shard_map/convert_element_type | solution.py:529
  421.3 69.4 %weight_ag.1 = bf16[4,4,4,1024,128]{4,3,2,1,0:T(8,128)(2,1)} custom-call(bf16[1024,128]{1,0:T(8,128)(2,1)} %bitcast.47), custom_call_target="tpu_custom_call" | custom-call | tf_op jit(solution)/shard_map/weight_ag/pallas_call | solution.py:354
  490.7 51.1 %flatten.1 = bf16[1,8388608]{1,0:T(2,128)(2,1)} custom-call(bf16[65536,128]{1,0:T(8,128)(2,1)} %bitcast.38), custom_call_target="tpu_custom_call" | custom-call | tf_op jit(solution)/shard_map/flatten/pallas_call | solution.py:445
Async XLA Ops:
  50.2 18.0 %copy-start = (bf16[4096,1024]{1,0:T(8,128)(2,1)S(1)}, bf16[4096,1024]{1,0:T(8,128)(2,1)}, u32[]{:S(2)}) copy-start(bf16[4096,1024]{1,0:T(8,128)(2,1)} %get-tuple-element.34) | copy-start | bytes 25165828 | tf_op jit(solution)/shard_map/cond
  50.2 18.0 %copy-start.2 = (bf16[1024,1024]{1,0:T(8,128)(2,1)S(1)}, bf16[1024,1024]{1,0:T(8,128)(2,1)}, u32[]{:S(2)}) copy-start(bf16[1024,1024]{1,0:T(8,128)(2,1)} %get-tuple-element.32) | copy-start | bytes 6291460 | tf_op jit(solution)/shard_map/cond
  79.7 5.1 collective-permute-start
  102.5 1.3 copy-start.7
  103.8 57.3 %collective-permute-start.1 = (bf16[1024,1024]{1,0:T(8,128)(2,1)}, bf16[1024,1024]{1,0:T(8,128)(2,1)S(1)}, u32[]{:S(2)}, u32[]{:S(2)}) collective-permute-start(bf16[1024,1024]{1,0:T(8,128)(2,1)} %copy-done.7), channel_id=1, source_target_pairs={{64,0},{65,1},{66,2},{67,3},{68,4},{69,5},{70,6},{71,7},{72,8},{73... | collective-permute-start | bytes 6291464 | tf_op jit(solution)/shard_map/ppermute | solution.py:518
  217.3 192.4 %copy-start.3 = (f32[1,1,131072]{2,1,0:T(1,128)S(1)}, f32[1,1,131072]{2,1,0:T(1,128)}, u32[]{:S(2)}) copy-start(f32[1,1,131072]{2,1,0:T(1,128)} %param.16) | copy-start | bytes 1572868
  217.3 192.4 %copy-start.4 = (f32[1,1,131072]{2,1,0:T(1,128)S(1)}, f32[1,1,131072]{2,1,0:T(1,128)}, u32[]{:S(2)}) copy-start(f32[1,1,131072]{2,1,0:T(1,128)} %param.17) | copy-start | bytes 1572868
  217.3 192.4 %copy-start.5 = (f32[1,1,131072]{2,1,0:T(1,128)S(1)}, f32[1,1,131072]{2,1,0:T(1,128)}, u32[]{:S(2)}) copy-start(f32[1,1,131072]{2,1,0:T(1,128)} %param.18) | copy-start | bytes 1572868

commit v2 on v1

v2 whole, which is shorter than its diff:
```python
import functools
import math
import jax
import jax.numpy as jnp
from jax import lax
from jax.experimental import pallas as pl
from jax.experimental.pallas import tpu as pltpu
from jax.sharding import PartitionSpec as P

ADAM_BETA1 = 0.9
ADAM_BETA2 = 0.95
ADAM_EPS = 1e-8
WEIGHT_DECAY = 0.1
ADAM_STEP = 10
LR_BASE = 0.05
MESH = pl.DeviceIdType.MESH
MIB = 1024 * 1024

SUBS = 4
SUB_ROWS = 256
ALL = slice(None)
RING = pl.ds(0, 4)
BOTH = range(2)
AXES = range(3)
LEADS = (16, 4, 1)
ROWWISE = ((0,), (0,))
DELTAS = (1, -1)
RS_ORDER = ((2, 1, 0), (1, 0, 2), (0, 2, 1))
UNIT_SHIFT = {2: 0, 3: -1, 4: 1, 5: 2}
AG_ORDER = ((0, 1, 2), (1, 2, 0), (2, 0, 1))


def upto(n):
    return pl.ds(0, n)


def divide(t):
    return t // 4, lax.rem(t, 4)


def wrap(k):
    return lax.rem(k + 4, 4)


def rs_split():
    table = {}
    for s in range(SUBS):
        sizes = [11, 11, 11]
        sizes[(s + 2) % 3] = 10
        start = 32 * s
        for c in AXES:
            n = sizes[c]
            first = (n + (s + c) % 2) // 2
            table[s, c] = tuple(8 * k for k in (start, first, n - first))
            start += n
    return table


def coords_of(me):
    return [me // 16, lax.rem(me // 4, 4), lax.rem(me, 4)]


def peer(coords, pos, delta):
    moved = list(coords)
    moved[pos] = wrap(coords[pos] + delta)
    z, y, x = moved
    return z * 16 + y * 4 + x


def greet(coords, deltas, partner):
    barrier = pltpu.get_barrier_semaphore()
    ids = [{"data": peer(coords, pos, delta)} for pos in AXES for delta in deltas]
    if partner:
        ids.append({"stage": 1 - lax.axis_index("stage")})
    for other in ids:
        pl.semaphore_signal(barrier, inc=1, device_id=other, device_id_type=MESH)
    pl.semaphore_wait(barrier, len(ids))


def sum_everywhere(coords, acc, got, ssem, rsem):
    copies = []
    for ph in range(4):
        if ph < 3:
            mine = coords[ph]
            targets = [{"data": peer(coords, ph, k)} for k in range(1, 4)]
        else:
            mine = lax.axis_index("stage")
            targets = [{"stage": 1 - mine}]
        batch = []
        for k, target in enumerate(targets):
            i = ph * 3 + k
            batch.append(pltpu.make_async_remote_copy(src_ref=acc.at[ph], dst_ref=got.at[ph, mine], send_sem=ssem.at[i],
                                                      recv_sem=rsem.at[i], device_id=target, device_id_type=MESH))
        for copy in batch:
            copy.start()
        got[ph, mine] = acc[ph]
        for copy in batch:
            copy.wait_recv()
        acc[ph + 1] = sum(got[ph, k] for k in range(len(batch) + 1))
        copies += batch
    for copy in copies:
        copy.wait_send()


def rs_kernel(g_ref, loss_ref, out_ref, total_ref, ra1, rb1, lb, own, ra2, rb2, ra3, rb3, ssem, rsem, lsem, acc, got, tsem, usem):
    coords = coords_of(lax.axis_index("data"))
    table = rs_split()
    ra = (ra1, ra2, ra3)
    rb = (rb1, rb2, rb3)
    copies = {}

    def rows(s, c, half):
        start, n0, n1 = table[s, c]
        if half == 0:
            return 0, n0
        if half == 1:
            return n0, n1
        return 0, n0 + n1

    def lead(ph, c, k):
        order = RS_ORDER[c]
        left = [p for p in AXES if p != order[0]]
        idx = []
        for p in left:
            if ph == 1:
                idx.append(k if p == order[1] else RING)
            else:
                idx.append(coords[order[1]] if p == order[1] else k)
        return tuple(idx)

    def lead_t(ph, c, k, t):
        if ph == 0:
            return divide(t), divide(t)
        mine = tuple(t if i is RING else i for i in lead(ph, c, k))
        return (t,) * (2 - ph), mine

    def source(ph, s, c, k, half):
        lo, n = rows(s, c, half)
        if ph == 0:
            idx = [RING] * 3
            idx[RS_ORDER[c][0]] = k
            return g_ref.at[tuple(idx) + (pl.ds(table[s, c][0] + lo, n), ALL)]
        return own.at[(s * 3 + c,) + lead(ph, c, k) + (pl.ds(lo, n), ALL)]

    def slot(ref, ph, i, lo, n):
        return ref.at[(i,) + (RING,) * (2 - ph) + (pl.ds(lo, n), ALL)]

    def start(ph, s, c, d, piece, src, dst):
        i = (((ph * SUBS + s) * 3 + c) * 2 + d) * 3 + piece
        target = peer(coords, RS_ORDER[c][ph], DELTAS[d])
        copy = pltpu.make_async_remote_copy(src_ref=src, dst_ref=dst, send_sem=ssem.at[i], recv_sem=rsem.at[i],
                                            device_id={"data": target}, device_id_type=MESH)
        copy.start()
        copies[ph, s, c, d, piece] = copy

    def at(c, ph, delta):
        return wrap(coords[RS_ORDER[c][ph]] + delta)

    def send_a(ph, s, c):
        for d in BOTH:
            n = rows(s, c, d)[1]
            start(ph, s, c, d, 0, source(ph, s, c, at(c, ph, 2), d), slot(ra[ph], ph, s * 6 + c * 2 + d, 0, n))

    def send_b1(ph, s, c):
        for d in BOTH:
            lo, n = rows(s, c, 1 - d)
            start(ph, s, c, d, 1, source(ph, s, c, at(c, ph, DELTAS[d]), 1 - d), slot(rb[ph], ph, s * 6 + c * 2 + d, lo, n))

    def load(s, c):
        for d in BOTH:
            i = s * 9 + c * 3 + d
            n = rows(s, c, d)[1]
            copy = pltpu.make_async_copy(source(0, s, c, at(c, 0, DELTAS[d]), d), slot(lb, 0, s * 6 + c * 2 + d, 0, n), lsem.at[i])
            copy.start()
            copies["lb", s, c, d] = copy
        n = rows(s, c, 2)[1]
        copy = pltpu.make_async_copy(source(0, s, c, at(c, 0, 0), 2), slot(own, 0, s * 3 + c, 0, n), lsem.at[s * 9 + c * 3 + 2])
        copy.start()
        copies["own", s, c] = copy

    def forward(ph, s, c):
        for d in BOTH:
            i = s * 6 + c * 2 + d
            lo, n = rows(s, c, d)
            if ph == 0:
                copies["lb", s, c, d].wait()
            copies[ph, s, c, d, 0].wait_recv()
            buf = ra[ph]
            k = at(c, ph, DELTAS[d])

            def body(t, carry, i=i, n=n, lo=lo, buf=buf, k=k):
                where, mine = lead_t(ph, c, k, t)
                term = lb[(i,) + where + (upto(n), ALL)] if ph == 0 else own[(s * 3 + c,) + mine + (pl.ds(lo, n), ALL)]
                buf[(i,) + where + (upto(n), ALL)] += term
                return carry

            lax.fori_loop(0, LEADS[ph], body, 0)
            start(ph, s, c, d, 2, slot(buf, ph, i, 0, n), slot(rb[ph], ph, i, lo, n))

    def finish(ph, s, c):
        if ph == 0:
            copies["own", s, c].wait()
        for d in BOTH:
            copies[ph, s, c, d, 1].wait_recv()
            copies[ph, s, c, d, 2].wait_recv()
        n = rows(s, c, 2)[1]
        i, j = s * 6 + c * 2, s * 3 + c
        buf = rb[ph]
        k = at(c, ph, 0)
        span = upto(n)

        def body(t, carry):
            where, mine = lead_t(ph, c, k, t)
            mine = (j,) + mine + (span, ALL)
            total = own[mine] + buf[(i,) + where + (span, ALL)] + buf[(i + 1,) + where + (span, ALL)]
            if ph < 2:
                own[mine] = total
            else:
                out_ref[pl.ds(table[s, c][0], n), :] = total
            return carry

        lax.fori_loop(0, LEADS[ph], body, 0)

    def st0(s):
        for c in AXES:
            send_a(0, s, c)
            load(s, c)

    def st0b(s):
        for c in AXES:
            send_b1(0, s, c)

    def mid(ph, s):
        for c in AXES:
            forward(ph, s, c)

    def turn(ph, s):
        for c in AXES:
            finish(ph, s, c)
            if ph < 2:
                send_a(ph + 1, s, c)
                send_b1(ph + 1, s, c)

    def opening(s):
        if s < SUBS:
            st0(s)

    def second(s):
        if s < SUBS:
            st0b(s)

    steps = []
    for s in range(SUBS):
        done = 3 * s + 4
        steps.append((max(s, 3 * s - 1), 0, mid, 0, s))
        for ph in AXES:
            steps.append((done + 4 * ph, 1, turn, ph, s))
            if ph:
                steps.append((done + 4 * ph - 2, 1, mid, ph, s))
    greet(coords, range(1, 4), True)
    opening(0)
    opening(1)
    second(0)
    for _, _, act, ph, s in sorted(steps, key=lambda e: e[:2]):
        act(ph, s)
        if act is mid and ph == 0:
            opening(s + 2)
            second(s + 1)
    for key, copy in copies.items():
        if not isinstance(key[0], str):
            copy.wait_send()
    part = out_ref[...]
    acc[0, 0] = jnp.sum((part * part).reshape(-1, 8, 128), axis=0)
    acc[0, 1] = loss_ref[...]
    sum_everywhere(coords, acc, got, tsem, usem)
    total_ref[...] = acc[4]


def reduce_scatter(g, loss):
    sems = 54 * SUBS
    f32 = jnp.float32
    dma = pltpu.SemaphoreType.DMA
    vmem = pl.BlockSpec(memory_space=pltpu.VMEM)

    def slots(n, axes, rows):
        return pltpu.VMEM((SUBS * n,) + (4,) * axes + (rows, 128), f32)

    return pl.pallas_call(
        rs_kernel,
        out_shape=(jax.ShapeDtypeStruct((1024, 128), f32), jax.ShapeDtypeStruct((2, 8, 128), f32)),
        in_specs=[pl.BlockSpec(memory_space=pl.ANY), vmem],
        out_specs=(vmem, vmem),
        scratch_shapes=[slots(6, 2, 48), slots(6, 2, 88), slots(6, 2, 48), slots(3, 2, 88), slots(6, 1, 48), slots(6, 1, 88),
                        slots(6, 0, 48), slots(6, 0, 88), dma((sems,)), dma((sems,)), dma((SUBS * 9,)),
                        pltpu.VMEM((5, 2, 8, 128), f32), pltpu.VMEM((4, 4, 2, 8, 128), f32), dma((10,)), dma((10,))],
        compiler_params=pltpu.CompilerParams(collective_id=0, has_side_effects=True, vmem_limit_bytes=60 * MIB),
        name="grad_rs",
    )(g, loss)


def ag_split():
    table = []
    start = 0
    for c, n in enumerate((22, 21, 21)):
        first = (n + c % 2) // 2
        table.append(tuple(16 * k for k in (start, first, n - first)))
        start += n
    return table


def ag_kernel(w_ref, wide_ref, out_ref, stage, ssem, rsem, lsem):
    coords = coords_of(lax.axis_index("data"))
    table = ag_split()
    copies = {}

    def rows(c, half):
        start, n0, n1 = table[c]
        return (start, n0) if half == 0 else (start + n0, n1)

    def region(c, unit, shift, half):
        first, second, third = AG_ORDER[c]
        idx = [None] * 3
        if unit == 0:
            idx[first], idx[second], idx[third] = wrap(coords[first] + shift), coords[second], coords[third]
        elif unit == 1:
            idx[first], idx[second], idx[third] = RING, wrap(coords[second] + shift), coords[third]
        else:
            q = wrap(coords[second] + UNIT_SHIFT[unit])
            idx[first], idx[second], idx[third] = RING, q, wrap(coords[third] + shift)
        lo, n = rows(c, half)
        return out_ref.at[tuple(idx) + (pl.ds(lo, n), ALL)]

    def start(c, unit, d, piece, src, dst):
        i = ((unit * 3 + c) * 2 + d) * 3 + piece
        target = peer(coords, AG_ORDER[c][min(unit, 2)], DELTAS[d])
        copy = pltpu.make_async_remote_copy(src_ref=src, dst_ref=dst, send_sem=ssem.at[i], recv_sem=rsem.at[i],
                                            device_id={"data": target}, device_id_type=MESH)
        copy.start()
        copies[c, unit, d, piece] = copy

    def begin(unit):
        for c in AXES:
            for d in BOTH:
                for piece, half in ((0, d), (1, 1 - d)):
                    lo, n = rows(c, half)
                    here = region(c, unit, 0, half)
                    src = w_ref.at[pl.ds(lo, n), :] if unit == 0 else here
                    start(c, unit, d, piece, src, here)

    def middle(unit):
        for c in AXES:
            for d in BOTH:
                copies[c, unit, d, 0].wait_recv()
                part = region(c, unit, -DELTAS[d], d)
                start(c, unit, d, 2, part, part)

    def arrive(unit, piece):
        for c in AXES:
            for d in BOTH:
                copies[c, unit, d, piece].wait_recv()

    flights = []

    def widen(unit):
        for c in AXES:
            start, n0, n1 = table[c]
            n = n0 + n1
            second = AG_ORDER[c][1]
            q = wrap(coords[second] + UNIT_SHIFT[unit])
            i = len(flights)
            if i > 1:
                flights[i - 2].wait()

            def body(t, carry):
                u, v = divide(t)
                where = [u, v]
                where.insert(second, q)
                stage[i % 2, u, v, upto(n), :] = out_ref[tuple(where) + (pl.ds(start, n), ALL)].astype(jnp.float32)
                return carry

            lax.fori_loop(0, 16, body, 0)
            where = [RING] * 2
            where.insert(second, q)
            flights.append(pltpu.make_async_copy(stage.at[i % 2, :, :, upto(n), :],
                                                 wide_ref.at[tuple(where) + (pl.ds(start, n), ALL)], lsem.at[i]))
            flights[i].start()

    greet(coords, DELTAS, False)
    begin(0)
    out_ref[tuple(coords)] = w_ref[...]
    middle(0)
    arrive(0, 1)
    arrive(0, 2)
    begin(1)
    begin(2)
    middle(1)
    arrive(1, 1)
    begin(3)
    begin(4)
    middle(2)
    arrive(1, 2)
    begin(5)
    middle(3)
    middle(4)
    middle(5)
    for unit in UNIT_SHIFT:
        arrive(unit, 1)
        arrive(unit, 2)
        widen(unit)
    for flight in flights[-2:]:
        flight.wait()
    for copy in copies.values():
        copy.wait_send()


def all_gather_rows(w):
    dma = pltpu.SemaphoreType.DMA
    sems = 36 * 3
    return pl.pallas_call(
        ag_kernel,
        out_shape=jax.ShapeDtypeStruct((4, 4, 4, 1024, 128), jnp.float32),
        in_specs=[pl.BlockSpec(memory_space=pltpu.VMEM)],
        out_specs=pl.BlockSpec(memory_space=pl.ANY),
        scratch_shapes=[pltpu.VMEM((4, 4, 4, 1024, 128), w.dtype), pltpu.VMEM((2, 4, 4, 352, 128), jnp.float32),
                        dma((sems,)), dma((sems,)), dma((12,))],
        compiler_params=pltpu.CompilerParams(collective_id=1, has_side_effects=True, vmem_limit_bytes=40 * MIB),
        name="weight_ag",
    )(w)


def wgrad_kernel(x_ref, du_ref, a_ref, g_ref, out_ref):
    part = pl.program_id(1)

    @pl.when(part == 0)
    def _():
        def body(m, carry):
            cols = pl.ds(pl.multiple_of(m * 256, 256), 256)
            val = lax.dot_general(x_ref[:, cols], du_ref[...], (ROWWISE, ((), ())), preferred_element_type=jnp.float32)
            for ct in range(8):
                out_ref[pl.ds(m * 8, 8), ct * 32:(ct + 1) * 32, :] = val[:, ct * 128:(ct + 1) * 128].reshape(8, 32, 128)
            return carry
        lax.fori_loop(0, 4, body, 0)

    @pl.when(part == 1)
    def _():
        def body(m, carry):
            cols = pl.ds(pl.multiple_of(m * 1024, 1024), 1024)
            val = lax.dot_general(a_ref[:, cols], g_ref[...], (ROWWISE, ((), ())), preferred_element_type=jnp.float32)
            for ct in BOTH:
                out_ref[pl.ds(m * 8, 8), ct * 128:(ct + 1) * 128, :] = val[:, ct * 128:(ct + 1) * 128].reshape(8, 128, 128)
            return carry
        lax.fori_loop(0, 4, body, 0)


def weight_grads(x, du, a, g):
    rows, d = x.shape
    return pl.pallas_call(
        wgrad_kernel,
        grid=(SUBS, 2),
        out_shape=jax.ShapeDtypeStruct((64, 1024, 128), jnp.float32),
        in_specs=[
            pl.BlockSpec((rows, d), lambda s, p: (0, 0)),
            pl.BlockSpec((rows, d), lambda s, p: (0, s)),
            pl.BlockSpec((rows, 4 * d), lambda s, p: (0, 0)),
            pl.BlockSpec((rows, d // 4), lambda s, p: (0, s)),
        ],
        out_specs=pl.BlockSpec((32, SUB_ROWS, 128), lambda s, p: (p, s, 0)),
        compiler_params=pltpu.CompilerParams(vmem_limit_bytes=56 * MIB, dimension_semantics=("arbitrary", "arbitrary")),
        cost_estimate=pl.CostEstimate(flops=4 * rows * d * 4 * d, bytes_accessed=52 * MIB, transcendentals=0),
        name="wgrad",
    )(x, du, a, g)


ROWS = 1024
WIDE = 4096
TILE = 256
COLS = 512
LANES = 128
STEPS = ROWS // TILE
PIECE = 131072
CHUNK = 4 * PIECE
CHUNKS = 2 * ROWS * WIDE // CHUNK
SLOTS = 4
PITCH = 40
GELU_A = math.sqrt(2.0 / math.pi)
GELU_B = GELU_A * 0.044715
BF16 = jnp.bfloat16
F32 = jnp.float32


def dot32(a, b, dims=((1,), (0,))):
    return lax.dot_general(a, b, (dims, ((), ())), preferred_element_type=F32)


def dot_t(a, b):
    return dot32(a, b, ((1,), (1,)))


def block_kernel(scale, w_ref, xin_ref, t_ref, x_out, a_out, du_out, g_out, loss_ref,
                 w1, w2, xb, hb, gb, ab, db, tb, raw, wide, wsem, insem, outsem, hs, hr, gs, gr):
    stage = lax.axis_index("stage")
    first = stage == 0
    last = stage == 1
    other = {"stage": 1 - stage}

    def chunk(i):
        return pltpu.make_async_copy(w_ref.at[:, pl.ds(pl.multiple_of(i * CHUNK, CHUNK), CHUNK)], raw.at[lax.rem(i, SLOTS)],
                                     wsem.at[lax.rem(i, SLOTS)])

    load_x = pltpu.make_async_copy(xin_ref, xb, insem.at[0])
    load_t = pltpu.make_async_copy(t_ref, tb, insem.at[1])

    def prefetch(i, carry):
        chunk(i).start()
        return carry

    lax.fori_loop(0, SLOTS, prefetch, 0)

    @pl.when(first)
    def _():
        load_x.start()

    @pl.when(last)
    def _():
        load_t.start()

    barrier = pltpu.get_barrier_semaphore()
    pl.semaphore_signal(barrier, inc=1, device_id=other, device_id_type=MESH)
    pl.semaphore_wait(barrier, 1)

    def convert(i, weight, blocks, pitch):
        rows = PIECE // (blocks * LANES)
        chunk(i).wait()

        def body(q, carry):
            for j in range(PIECE // ROWS):
                line = raw[lax.rem(i, SLOTS), :, pl.ds(pl.multiple_of(q * PIECE + j * ROWS, ROWS), ROWS)]
                at = (j * 8 // blocks) * pitch + j * 8 % blocks
                wide[at:at + 8, :] = line.astype(F32).reshape(8, LANES)
            base = pl.ds(pl.multiple_of((lax.rem(i, CHUNKS // 2) * 4 + q) * rows, rows), rows)
            for cb in range(blocks):
                weight[base, cb * LANES:(cb + 1) * LANES] = wide[pl.ds(cb, rows, stride=pitch), :].astype(BF16)
            return carry

        lax.fori_loop(0, 4, body, 0)

        @pl.when(i < CHUNKS - SLOTS)
        def _():
            chunk(i + SLOTS).start()

    def convert_first(i, carry):
        convert(i, w1, WIDE // LANES, PITCH)
        return carry

    def convert_second(i, carry):
        convert(i, w2, ROWS // LANES, ROWS // LANES)
        return carry

    lax.fori_loop(0, CHUNKS // 2, convert_first, 0)
    lax.fori_loop(CHUNKS // 2, CHUNKS, convert_second, 0)

    @pl.when(first)
    def _():
        load_x.wait()

    @pl.when(last)
    def _():
        load_t.wait()

    def span(i):
        return pl.ds(pl.multiple_of(i * TILE, TILE), TILE)

    def cols(j):
        return pl.ds(pl.multiple_of(j * COLS, COLS), COLS)

    def send_h(i):
        return pltpu.make_async_remote_copy(src_ref=hb.at[span(i)], dst_ref=xb.at[span(i)], send_sem=hs.at[i], recv_sem=hr.at[i],
                                            device_id=other, device_id_type=MESH)

    def send_g(i):
        return pltpu.make_async_remote_copy(src_ref=hb.at[span(i)], dst_ref=gb.at[span(i)], send_sem=gs.at[i], recv_sem=gr.at[i],
                                            device_id=other, device_id_type=MESH)

    def outputs(i):
        pairs = ((xb, x_out), (ab, a_out), (db, du_out), (gb, g_out))
        return [pltpu.make_async_copy(src.at[span(i)], dst.at[span(i)], outsem.at[i * 4 + k]) for k, (src, dst) in enumerate(pairs)]

    def forward(i):
        def up(j, carry):
            u = dot32(xb[span(i), :], w1[:, cols(j)]).astype(BF16)
            db[span(i), cols(j)] = u
            uf = u.astype(F32)
            half = 0.5 * uf
            ab[span(i), cols(j)] = (half + half * jnp.tanh(uf * (GELU_A + GELU_B * (uf * uf)))).astype(BF16)
            return carry

        def down(j, carry):
            hb[span(i), cols(j)] = (xb[span(i), cols(j)].astype(F32) + dot32(ab[span(i), :], w2[:, cols(j)])).astype(BF16)
            return carry

        lax.fori_loop(0, WIDE // COLS, up, 0, unroll=2)
        lax.fori_loop(0, ROWS // COLS, down, 0)

    def top(i):
        res = hb[span(i), :].astype(F32) - tb[span(i), :].astype(F32)
        gb[span(i), :] = (res * scale).astype(BF16)
        sums = jnp.sum((res * res).reshape(-1, 8, ROWS), axis=0)
        loss_ref[...] += sum(sums[:, k * LANES:(k + 1) * LANES] for k in range(ROWS // LANES))

    def backward(i):
        def body(j, carry):
            e = dot_t(gb[span(i), :], w2[cols(j), :])
            u = db[span(i), cols(j)].astype(F32)
            sq = u * u
            t = jnp.tanh(u * (GELU_A + GELU_B * sq))
            slope = 0.5 * (1.0 + t) + (0.5 * u) * (1.0 - t * t) * (GELU_A + (3.0 * GELU_B) * sq)
            db[span(i), cols(j)] = (e * slope).astype(BF16)
            return carry

        lax.fori_loop(0, WIDE // COLS, body, 0, unroll=2)

    def below(i):
        def body(j, carry):
            hb[span(i), cols(j)] = (gb[span(i), cols(j)].astype(F32) + dot_t(db[span(i), :], w1[cols(j), :])).astype(BF16)
            return carry

        lax.fori_loop(0, ROWS // COLS, body, 0)

    loss_ref[...] = jnp.zeros_like(loss_ref)

    def tick(it, carry):
        i = lax.rem(it, STEPS)

        @pl.when(it < STEPS)
        def _():
            @pl.when(last)
            def _():
                send_h(i).wait_recv()

            forward(i)

            @pl.when(first)
            def _():
                send_h(i).start()

            @pl.when(last)
            def _():
                top(i)

        @pl.when(it // STEPS + stage == 1)
        def _():
            @pl.when(first)
            def _():
                send_g(i).wait_recv()

            backward(i)

            @pl.when(last)
            def _():
                below(i)
                send_g(i).start()

            for copy in outputs(i):
                copy.start()
        return carry

    lax.fori_loop(0, 2 * STEPS, tick, 0)

    def drain(i, carry):
        @pl.when(first)
        def _():
            send_h(i).wait_send()

        @pl.when(last)
        def _():
            send_g(i).wait_send()

        for copy in outputs(i):
            copy.wait()
        return carry

    lax.fori_loop(0, STEPS, drain, 0)


def block_passes(flat, x_in, targets, token_count):
    anywhere = pl.BlockSpec(memory_space=pl.ANY)
    dma = pltpu.SemaphoreType.DMA
    narrow, wide = (ROWS, ROWS), (ROWS, WIDE)

    def shape(dims):
        return jax.ShapeDtypeStruct(dims, BF16)

    def room(dims):
        return pltpu.VMEM(dims, BF16)

    return pl.pallas_call(
        functools.partial(block_kernel, 1.0 / token_count),
        out_shape=(shape(narrow), shape(wide), shape(wide), shape(narrow), jax.ShapeDtypeStruct((8, LANES), F32)),
        in_specs=[anywhere] * 3,
        out_specs=(anywhere,) * 4 + (pl.BlockSpec(memory_space=pltpu.VMEM),),
        scratch_shapes=[room(wide), room((WIDE, ROWS)), room(narrow), room(narrow), room(narrow), room(wide), room(wide), room(narrow),
                        room((SLOTS, 1, CHUNK)), pltpu.VMEM((32 * PITCH, LANES), F32),
                        dma((SLOTS,)), dma((2,)), dma((STEPS * 4,)), dma((STEPS,)), dma((STEPS,)), dma((STEPS,)), dma((STEPS,))],
        compiler_params=pltpu.CompilerParams(collective_id=2, has_side_effects=True, vmem_limit_bytes=60 * MIB),
        name="block",
    )(flat, x_in, targets)


def adam_kernel(rate, token_count, part_ref, total_ref, tau_ref, w_ref, m_ref, v_ref, w_out, m_out, v_out, b_out, loss_out, grad):
    early = lax.axis_index("data") < 32

    def reorder(rows):
        blocks = ROWS // rows
        for r in range(rows):
            grad[r * blocks:(r + 1) * blocks, :] = part_ref[pl.ds(r, blocks, stride=rows), :]

    @pl.when(early)
    def _():
        reorder(32)

    @pl.when(jnp.logical_not(early))
    def _():
        reorder(LANES)

    nu = jnp.sqrt(jnp.sum(total_ref[0], keepdims=True))
    scaled = jnp.minimum(1.0, tau_ref[...] / nu) * grad[...]
    m_new = ADAM_BETA1 * m_ref[...] + (1.0 - ADAM_BETA1) * scaled
    v_new = ADAM_BETA2 * v_ref[...] + (1.0 - ADAM_BETA2) * scaled * scaled
    m_hat = m_new / (1.0 - ADAM_BETA1 ** ADAM_STEP)
    v_hat = v_new / (1.0 - ADAM_BETA2 ** ADAM_STEP)
    w_new = w_ref[...] - rate * (m_hat / (jnp.sqrt(v_hat) + ADAM_EPS) + WEIGHT_DECAY * w_ref[...])
    w_out[...] = w_new
    m_out[...] = m_new
    v_out[...] = v_new
    b_out[...] = w_new.astype(BF16)
    loss_out[...] = (0.5 * jnp.sum(total_ref[1], keepdims=True)) / token_count


def adam(rate, token_count, part, totals, tau, w, m, v):
    state = jax.ShapeDtypeStruct(part.shape, F32)
    vmem = pl.BlockSpec(memory_space=pltpu.VMEM)
    return pl.pallas_call(
        functools.partial(adam_kernel, rate, token_count),
        out_shape=(state, state, state, jax.ShapeDtypeStruct(part.shape, BF16), jax.ShapeDtypeStruct((1, 1), F32)),
        in_specs=[vmem] * 6,
        out_specs=(vmem,) * 5,
        scratch_shapes=[pltpu.VMEM(part.shape, F32)],
        name="adam",
    )(part, totals, tau, w, m, v)


def solution(mesh):
    data_size = mesh.shape['data']

    def device_step(x_in, targets, w_work, w_master, m_prior, v_prior, clip_tau):
        token_count = x_in.shape[0] * x_in.shape[1] * data_size
        x, a, du, g, loss = block_passes(w_work.reshape(1, -1), x_in.reshape(ROWS, ROWS), targets.reshape(ROWS, ROWS), token_count)
        grads = weight_grads(x, du, a, g)
        part, totals = reduce_scatter(grads.reshape(4, 4, 4, ROWS, LANES), loss)
        rate = LR_BASE / math.sqrt(x_in.shape[-1])
        state = [z.reshape(ROWS, LANES) for z in (w_master, m_prior, v_prior)]
        w_new, m_new, v_new, w_bf, loss_mean = adam(rate, token_count, part, totals, clip_tau.reshape(1, 1), *state)
        w_all = lax.optimization_barrier(all_gather_rows(w_bf).reshape(w_work.shape)).astype(BF16)
        return (loss_mean.reshape(()), w_all) + tuple(z.reshape(w_master.shape) for z in (w_new, m_new, v_new))

    row_spec = P(None, 'data', None)
    shard_spec = P('stage', None, 'data')
    stage_spec = P('stage', None, None)
    return jax.shard_map(device_step, mesh=mesh, in_specs=(row_spec, row_spec, stage_spec, shard_spec, shard_spec, shard_spec, P()), out_specs=(P(), stage_spec, shard_spec, shard_spec, shard_spec), check_vma=False)
```

time: 554 us -> 378 us (0.68); the launches traced: 544 us -> 378 us
  blocking collectives: 63.2 us -> 0 us
  waiting for transfers between devices: 57.8 us -> 0 us
  matrix products: 52 us -> 0 us
  Pallas kernels: 325 us -> 349 us
  local copies, waits for them, and re-layouts: 15.3 us -> 0.95 us
  other arithmetic: 14.1 us -> 26.4 us
  loops' own time: 8.48 us -> 0 us
    psum x1 -> x0, blocking collectives: 63.2 us -> none  [device_step(): lax.psum(jnp.stack([jnp.sum(part * part), loss_acc]), ('stage', 'data'))]
    ppermute x2 -> x0, waiting for transfers between devices: 57.8 us -> none  [the longest x1 55.4 us: device_step(): g_recv = lax.ppermute(g_in, 'stage', [(1, 0)])]
    dot_general x3 -> x0, matrix products: 52 us -> none  [dot32(): lax.dot_general(a, b, (dims, ((), ())), preferred_element_type=jnp.float32)]
    pallas_call x4 -> x3, Pallas kernels: 223 us -> 243 us  [the longest x1 152 us: reduce_scatter(): pl.pallas_call(rs_kernel, out_shape=(jax.ShapeDtypeStruct((1024, 128), f3...]
    convert_element_type x1, other arithmetic: 11.6 us -> 26.4 us  [device_step(): lax.optimization_barrier(all_gather_rows(w_bf).reshape(w_work.shape))]
    another operation x3 -> x0, loops' own time: 8.48 us -> none  [the longest x1 8.47 us: device_step(): lax.cond(is_first, lambda: (x0, u0, a0, narrow, wide, narrow, jnp.zeros((...]
    broadcast_in_dim x3 -> x0, local copies, waits for them, and re-layouts: 6.16 us -> none  [the longest x1 4.27 us: device_step(): wide = jnp.zeros((rows, 4 * d), bf)]
  transfers between devices with their start and end apart: 2 -> 0, of which waited for: 2 -> 0; matrix products, arithmetic and copies ran while one was open for 0% -> 0% of each run, Pallas kernels for 0% -> 0%
where the time goes in v2:
time: 378 us
  Pallas kernels  349 us (92%)
  other arithmetic  26.4 us (7%)
    pallas_call x1, Pallas kernels, reduce_scatter(): pl.pallas_call(rs_kernel, out_shape=(jax.ShapeDtypeStruct((1024, 128), f3...  152 us
    pallas_call x1, Pallas kernels, block_passes(): pl.pallas_call(functools.partial(block_kernel, 1.0 / token_count), out_sh...  87.1 us
    pallas_call x1, Pallas kernels, all_gather_rows(): pl.pallas_call(ag_kernel, out_shape=jax.ShapeDtypeStruct((4, 4, 4, 1024,...  74.2 us
    pallas_call x1, Pallas kernels, weight_grads(): pl.pallas_call(wgrad_kernel, grid=(SUBS, 2), out_shape=jax.ShapeDtypeStru...  32.2 us
    convert_element_type x1, other arithmetic, device_step(): lax.optimization_barrier(all_gather_rows(w_bf).reshape(w_work.shape))  26.4 us

profile of v2, /device:TPU:0, one launch (start us, length us, event | category | flops | bytes accessed | tf_op | source)
XLA Modules:
  0.0 377.8 jit_solution(15939670599832214561)
XLA Ops:
  1.3 87.1 %block.1 = (bf16[1024,1024]{1,0:T(8,128)(2,1)}, bf16[1024,4096]{1,0:T(8,128)(2,1)}, bf16[1024,4096]{1,0:T(8,128)(2,1)}, bf16[1024,1024]{1,0:T(8,128)(2,1)}, f32[8,128]{1,0:T(8,128)}) custom-call(bf16[1,8388608]{1,0:T(2,128)(2,1)} %bitcast.15, bf16[1024,1024]{1,0:T(8,128)(2,1)} %bitcast.17, bf16[1024,1024]{1,0:T(8,128)(2,1)} %bitcast.18), custom_call_target="tpu_custom_call" | custom-call | tf_op jit(solution)/shard_map/block/pallas_call | solution.py:696
  88.4 32.2 %wgrad.1 = f32[64,1024,128]{2,1,0:T(8,128)} custom-call(bf16[1024,1024]{1,0:T(8,128)(2,1)} %get-tuple-element.17.x_ref, bf16[1024,4096]{1,0:T(8,128)(2,1)} %get-tuple-element.18.du_ref, bf16[1024,4096]{1,0:T(8,128)(2,1)} %get-tuple-element.19.a_ref, bf16[1024,1024]{1,0:T(8,128)(2,1)} %get-tuple-element.20.g_ref), custom_call_target="tpu_custom_call" | custom-call | flops 17179869184 | bytes 54525952 | tf_op jit(solution)/shard_map/wgrad/pallas_call | solution.py:457
  120.6 151.7 %grad_rs.1 = (f32[1024,128]{1,0:T(8,128)}, f32[2,8,128]{2,1,0:T(8,128)}) custom-call(f32[4,4,4,1024,128]{4,3,2,1,0:T(8,128)} %bitcast.16, f32[8,128]{1,0:T(8,128)} %get-tuple-element.21.loss_ref), custom_call_target="tpu_custom_call" | custom-call | tf_op jit(solution)/shard_map/grad_rs/pallas_call | solution.py:288
  272.3 3.9 %adam.1 = (f32[1024,128]{1,0:T(8,128)}, f32[1024,128]{1,0:T(8,128)}, f32[1024,128]{1,0:T(8,128)}, bf16[1024,128]{1,0:T(8,128)(2,1)}, f32[1,1]{1,0:T(1,128)}) custom-call(f32[1024,128]{1,0:T(8,128)} %get-tuple-element.22.part_ref, f32[2,8,128]{2,1,0:T(8,128)} %get-tuple-element.23.total_ref, f32[1,1]{1,0:T(1,128)} %bitcast.13.tau_ref, f32[1024,128]{1,0:T(8,128)} %bitcast.19, ...), custom_call_target="tpu_custom_call" | custom-call | tf_op jit(solution)/shard_map/adam/pallas_call | solution.py:742
  276.2 0.0 copy-start
  276.2 0.9 copy-done
  277.2 74.2 %weight_ag.1 = f32[4,4,4,1024,128]{4,3,2,1,0:T(8,128)} custom-call(bf16[1024,128]{1,0:T(8,128)(2,1)S(1)} %copy-done), custom_call_target="tpu_custom_call" | custom-call | tf_op jit(solution)/shard_map/weight_ag/pallas_call | solution.py:419
  351.4 26.4 %convert_element_type.3 = bf16[1,1,8388608]{2,1,0:T(2,128)(2,1)} convert(f32[1,1,8388608]{2,1,0:T(1,128)} %bitcast.14) | non-fusion elementwise | flops 8388608 | bytes 50331648 | tf_op jit(solution)/shard_map/convert_element_type | solution.py:763
Async XLA Ops:
  276.2 0.9 copy-start

commit v3 on v2

--- a/solution.py
+++ b/solution.py
@@ -28,6 +28,23 @@
 RS_ORDER = ((2, 1, 0), (1, 0, 2), (0, 2, 1))
 UNIT_SHIFT = {2: 0, 3: -1, 4: 1, 5: 2}
 AG_ORDER = ((0, 1, 2), (1, 2, 0), (2, 0, 1))
+
+
+ROWS = 1024
+WIDE = 4096
+TILE = 256
+COLS = 512
+LANES = 128
+STEPS = ROWS // TILE
+PIECE = 131072
+CHUNK = 4 * PIECE
+CHUNKS = 2 * ROWS * WIDE // CHUNK
+SLOTS = 4
+PITCH = 40
+GELU_A = math.sqrt(2.0 / math.pi)
+GELU_B = GELU_A * 0.044715
+BF16 = jnp.bfloat16
+F32 = jnp.float32
 
 
 def upto(n):
@@ -102,12 +119,77 @@
         copy.wait_send()
 
 
-def rs_kernel(g_ref, loss_ref, out_ref, total_ref, ra1, rb1, lb, own, ra2, rb2, ra3, rb3, ssem, rsem, lsem, acc, got, tsem, usem):
+def rs_kernel(x_ref, du_ref, a_ref, top_ref, loss_ref, out_ref, total_ref, g_ref, ra1, rb1, lb, own, ra2, rb2, ra3, rb3, ssem, rsem, lsem,
+              acc, got, tsem, usem, xb, gb, dub, ab, put1, put2, insem, dusem, asem, psem1, psem2):
     coords = coords_of(lax.axis_index("data"))
     table = rs_split()
     ra = (ra1, ra2, ra3)
     rb = (rb1, rb2, rb3)
     copies = {}
+
+    load_x = pltpu.make_async_copy(x_ref, xb, insem.at[0])
+    load_g = pltpu.make_async_copy(top_ref, gb, insem.at[1])
+
+    def load_du(s):
+        return pltpu.make_async_copy(du_ref.at[:, pl.ds(s * ROWS, ROWS)], dub.at[s % 2], dusem.at[s % 2])
+
+    def load_a(m):
+        return pltpu.make_async_copy(a_ref.at[:, pl.ds(pl.multiple_of(m * COLS, COLS), COLS)], ab.at[lax.rem(m, 2)], asem.at[lax.rem(m, 2)])
+
+    def grads(s):
+        band = pl.ds(s * SUB_ROWS, SUB_ROWS)
+        load_a(0).start()
+        if s + 1 < SUBS:
+            load_du(s + 1).start()
+        load_du(s).wait()
+        if s == 0:
+            load_x.wait()
+            load_g.wait()
+
+        def write1(m):
+            return pltpu.make_async_copy(put1.at[lax.rem(m, 2)], g_ref.at[m // 2, pl.ds(lax.rem(m, 2) * 2, 2), :, band, :],
+                                         psem1.at[lax.rem(m, 2)])
+
+        def write2(m):
+            return pltpu.make_async_copy(put2.at[lax.rem(m, 2)], g_ref.at[m // 4 + 2, lax.rem(m, 4), :, band, :],
+                                         psem2.at[lax.rem(m, 2)])
+
+        def first(m, carry):
+            val = dot32(xb[:, pl.ds(pl.multiple_of(m * TILE, TILE), TILE)], dub[s % 2], ROWWISE)
+
+            @pl.when(m > 1)
+            def _():
+                write1(m - 2).wait()
+
+            for ct in range(ROWS // LANES):
+                put1[lax.rem(m, 2), :, :, ct * 32:(ct + 1) * 32, :] = val[:, ct * LANES:(ct + 1) * LANES].reshape(2, 4, 32, LANES)
+            write1(m).start()
+            return carry
+
+        def second(m, carry):
+            load_a(m).wait()
+
+            @pl.when(m < 7)
+            def _():
+                load_a(m + 1).start()
+
+            val = dot32(ab[lax.rem(m, 2)], gb[:, band], ROWWISE)
+
+            @pl.when(m > 1)
+            def _():
+                write2(m - 2).wait()
+
+            for ct in BOTH:
+                part = slice(ct * LANES, (ct + 1) * LANES)
+                put2[lax.rem(m, 2), :, part, :] = val[:, part].reshape(4, LANES, LANES)
+            write2(m).start()
+            return carry
+
+        lax.fori_loop(0, 4, first, 0)
+        lax.fori_loop(0, 8, second, 0)
+        for m in BOTH:
+            write1(m + 2).wait()
+            write2(m + 6).wait()
 
     def rows(s, c, half):
         start, n0, n1 = table[s, c]
@@ -170,7 +252,7 @@
         for d in BOTH:
             i = s * 9 + c * 3 + d
             n = rows(s, c, d)[1]
-            copy = pltpu.make_async_copy(source(0, s, c, at(c, 0, DELTAS[d]), d), slot(lb, 0, s * 6 + c * 2 + d, 0, n), lsem.at[i])
+            copy = pltpu.make_async_copy(source(0, s, c, at(c, 0, DELTAS[d]), d), slot(lb, 0, s % 2 * 6 + c * 2 + d, 0, n), lsem.at[i])
             copy.start()
             copies["lb", s, c, d] = copy
         n = rows(s, c, 2)[1]
@@ -188,9 +270,9 @@
             buf = ra[ph]
             k = at(c, ph, DELTAS[d])
 
-            def body(t, carry, i=i, n=n, lo=lo, buf=buf, k=k):
+            def body(t, carry, d=d, i=i, n=n, lo=lo, buf=buf, k=k):
                 where, mine = lead_t(ph, c, k, t)
-                term = lb[(i,) + where + (upto(n), ALL)] if ph == 0 else own[(s * 3 + c,) + mine + (pl.ds(lo, n), ALL)]
+                term = lb[(s % 2 * 6 + c * 2 + d,) + where + (upto(n), ALL)] if ph == 0 else own[(s * 3 + c,) + mine + (pl.ds(lo, n), ALL)]
                 buf[(i,) + where + (upto(n), ALL)] += term
                 return carry
 
@@ -243,6 +325,7 @@
 
     def opening(s):
         if s < SUBS:
+            grads(s)
             st0(s)
 
     def second(s):
@@ -257,15 +340,18 @@
             steps.append((done + 4 * ph, 1, turn, ph, s))
             if ph:
                 steps.append((done + 4 * ph - 2, 1, mid, ph, s))
+    load_x.start()
+    load_du(0).start()
+    load_g.start()
     greet(coords, range(1, 4), True)
     opening(0)
+    second(0)
     opening(1)
-    second(0)
     for _, _, act, ph, s in sorted(steps, key=lambda e: e[:2]):
         act(ph, s)
         if act is mid and ph == 0:
+            second(s + 1)
             opening(s + 2)
-            second(s + 1)
     for key, copy in copies.items():
         if not isinstance(key[0], str):
             copy.wait_send()
@@ -276,26 +362,32 @@
     total_ref[...] = acc[4]
 
 
-def reduce_scatter(g, loss):
+def reduce_scatter(x, du, a, g, loss):
     sems = 54 * SUBS
     f32 = jnp.float32
     dma = pltpu.SemaphoreType.DMA
     vmem = pl.BlockSpec(memory_space=pltpu.VMEM)
-
-    def slots(n, axes, rows):
-        return pltpu.VMEM((SUBS * n,) + (4,) * axes + (rows, 128), f32)
-
-    return pl.pallas_call(
+    anywhere = pl.BlockSpec(memory_space=pl.ANY)
+
+    def slots(n, axes, rows, subs=SUBS):
+        return pltpu.VMEM((subs * n,) + (4,) * axes + (rows, LANES), f32)
+
+    part, totals, _ = pl.pallas_call(
         rs_kernel,
-        out_shape=(jax.ShapeDtypeStruct((1024, 128), f32), jax.ShapeDtypeStruct((2, 8, 128), f32)),
-        in_specs=[pl.BlockSpec(memory_space=pl.ANY), vmem],
-        out_specs=(vmem, vmem),
-        scratch_shapes=[slots(6, 2, 48), slots(6, 2, 88), slots(6, 2, 48), slots(3, 2, 88), slots(6, 1, 48), slots(6, 1, 88),
+        out_shape=(jax.ShapeDtypeStruct((ROWS, LANES), f32), jax.ShapeDtypeStruct((2, 8, LANES), f32),
+                   jax.ShapeDtypeStruct((4, 4, 4, ROWS, LANES), f32)),
+        in_specs=[anywhere] * 4 + [vmem],
+        out_specs=(vmem, vmem, anywhere),
+        scratch_shapes=[slots(6, 2, 48), slots(6, 2, 88), slots(6, 2, 48, 2), slots(3, 2, 88), slots(6, 1, 48), slots(6, 1, 88),
                         slots(6, 0, 48), slots(6, 0, 88), dma((sems,)), dma((sems,)), dma((SUBS * 9,)),
-                        pltpu.VMEM((5, 2, 8, 128), f32), pltpu.VMEM((4, 4, 2, 8, 128), f32), dma((10,)), dma((10,))],
-        compiler_params=pltpu.CompilerParams(collective_id=0, has_side_effects=True, vmem_limit_bytes=60 * MIB),
+                        pltpu.VMEM((5, 2, 8, LANES), f32), pltpu.VMEM((4, 4, 2, 8, LANES), f32), dma((10,)), dma((10,)),
+                        pltpu.VMEM((ROWS, ROWS), BF16), pltpu.VMEM((ROWS, ROWS), BF16), pltpu.VMEM((2, ROWS, ROWS), BF16),
+                        pltpu.VMEM((2, ROWS, COLS), BF16), pltpu.VMEM((2, 2, 4, SUB_ROWS, LANES), f32),
+                        pltpu.VMEM((2, 4, SUB_ROWS, LANES), f32), dma((2,)), dma((2,)), dma((2,)), dma((2,)), dma((2,))],
+        compiler_params=pltpu.CompilerParams(collective_id=0, has_side_effects=True, vmem_limit_bytes=63 * MIB),
         name="grad_rs",
-    )(g, loss)
+    )(x, du, a, g, loss)
+    return part, totals
 
 
 def ag_split():
@@ -428,66 +520,6 @@
     )(w)
 
 
-def wgrad_kernel(x_ref, du_ref, a_ref, g_ref, out_ref):
-    part = pl.program_id(1)
-
-    @pl.when(part == 0)
-    def _():
-        def body(m, carry):
-            cols = pl.ds(pl.multiple_of(m * 256, 256), 256)
-            val = lax.dot_general(x_ref[:, cols], du_ref[...], (ROWWISE, ((), ())), preferred_element_type=jnp.float32)
-            for ct in range(8):
-                out_ref[pl.ds(m * 8, 8), ct * 32:(ct + 1) * 32, :] = val[:, ct * 128:(ct + 1) * 128].reshape(8, 32, 128)
-            return carry
-        lax.fori_loop(0, 4, body, 0)
-
-    @pl.when(part == 1)
-    def _():
-        def body(m, carry):
-            cols = pl.ds(pl.multiple_of(m * 1024, 1024), 1024)
-            val = lax.dot_general(a_ref[:, cols], g_ref[...], (ROWWISE, ((), ())), preferred_element_type=jnp.float32)
-            for ct in BOTH:
-                out_ref[pl.ds(m * 8, 8), ct * 128:(ct + 1) * 128, :] = val[:, ct * 128:(ct + 1) * 128].reshape(8, 128, 128)
-            return carry
-        lax.fori_loop(0, 4, body, 0)
-
-
-def weight_grads(x, du, a, g):
-    rows, d = x.shape
-    return pl.pallas_call(
-        wgrad_kernel,
-        grid=(SUBS, 2),
-        out_shape=jax.ShapeDtypeStruct((64, 1024, 128), jnp.float32),
-        in_specs=[
-            pl.BlockSpec((rows, d), lambda s, p: (0, 0)),
-            pl.BlockSpec((rows, d), lambda s, p: (0, s)),
-            pl.BlockSpec((rows, 4 * d), lambda s, p: (0, 0)),
-            pl.BlockSpec((rows, d // 4), lambda s, p: (0, s)),
-        ],
-        out_specs=pl.BlockSpec((32, SUB_ROWS, 128), lambda s, p: (p, s, 0)),
-        compiler_params=pltpu.CompilerParams(vmem_limit_bytes=56 * MIB, dimension_semantics=("arbitrary", "arbitrary")),
-        cost_estimate=pl.CostEstimate(flops=4 * rows * d * 4 * d, bytes_accessed=52 * MIB, transcendentals=0),
-        name="wgrad",
-    )(x, du, a, g)
-
-
-ROWS = 1024
-WIDE = 4096
-TILE = 256
-COLS = 512
-LANES = 128
-STEPS = ROWS // TILE
-PIECE = 131072
-CHUNK = 4 * PIECE
-CHUNKS = 2 * ROWS * WIDE // CHUNK
-SLOTS = 4
-PITCH = 40
-GELU_A = math.sqrt(2.0 / math.pi)
-GELU_B = GELU_A * 0.044715
-BF16 = jnp.bfloat16
-F32 = jnp.float32
-
-
 def dot32(a, b, dims=((1,), (0,))):
     return lax.dot_general(a, b, (dims, ((), ())), preferred_element_type=F32)
 
@@ -612,8 +644,8 @@
             e = dot_t(gb[span(i), :], w2[cols(j), :])
             u = db[span(i), cols(j)].astype(F32)
             sq = u * u
-            t = jnp.tanh(u * (GELU_A + GELU_B * sq))
-            slope = 0.5 * (1.0 + t) + (0.5 * u) * (1.0 - t * t) * (GELU_A + (3.0 * GELU_B) * sq)
+            gate = 0.5 + 0.5 * jnp.tanh(u * (GELU_A + GELU_B * sq))
+            slope = gate + gate * ((1.0 - gate) * (u * (2.0 * GELU_A + (6.0 * GELU_B) * sq)))
             db[span(i), cols(j)] = (e * slope).astype(BF16)
             return carry
 
@@ -755,8 +787,7 @@
     def device_step(x_in, targets, w_work, w_master, m_prior, v_prior, clip_tau):
         token_count = x_in.shape[0] * x_in.shape[1] * data_size
         x, a, du, g, loss = block_passes(w_work.reshape(1, -1), x_in.reshape(ROWS, ROWS), targets.reshape(ROWS, ROWS), token_count)
-        grads = weight_grads(x, du, a, g)
-        part, totals = reduce_scatter(grads.reshape(4, 4, 4, ROWS, LANES), loss)
+        part, totals = reduce_scatter(x, du, a, g, loss)
         rate = LR_BASE / math.sqrt(x_in.shape[-1])
         state = [z.reshape(ROWS, LANES) for z in (w_master, m_prior, v_prior)]
         w_new, m_new, v_new, w_bf, loss_mean = adam(rate, token_count, part, totals, clip_tau.reshape(1, 1), *state)

time: 378 us -> 360 us (0.952)
  Pallas kernels: 349 us -> 331 us
    pallas_call x2 -> x1, Pallas kernels: 184 us -> 166 us  [reduce_scatter(): pl.pallas_call(rs_kernel, out_shape=(jax.ShapeDtypeStruct((ROWS, LANES),...]
where the time goes in v3:
time: 360 us; the launch traced here: 359 us
  Pallas kernels  331 us (92%)
  other arithmetic  26.4 us (7%)
    pallas_call x1, Pallas kernels, reduce_scatter(): pl.pallas_call(rs_kernel, out_shape=(jax.ShapeDtypeStruct((ROWS, LANES),...  166 us
    pallas_call x1, Pallas kernels, block_passes(): pl.pallas_call(functools.partial(block_kernel, 1.0 / token_count), out_sh...  86.5 us
    pallas_call x1, Pallas kernels, all_gather_rows(): pl.pallas_call(ag_kernel, out_shape=jax.ShapeDtypeStruct((4, 4, 4, 1024,...  74.5 us
    convert_element_type x1, other arithmetic, device_step(): lax.optimization_barrier(all_gather_rows(w_bf).reshape(w_work.shape))  26.4 us

profile of v3, /device:TPU:0, one launch (start us, length us, event | category | flops | bytes accessed | tf_op | source)
XLA Modules:
  0.0 359.2 jit_solution(6197438154923682170)
XLA Ops:
  1.3 86.5 %block.1 = (bf16[1024,1024]{1,0:T(8,128)(2,1)}, bf16[1024,4096]{1,0:T(8,128)(2,1)}, bf16[1024,4096]{1,0:T(8,128)(2,1)}, bf16[1024,1024]{1,0:T(8,128)(2,1)}, f32[8,128]{1,0:T(8,128)}) custom-call(bf16[1,8388608]{1,0:T(2,128)(2,1)} %bitcast.14, bf16[1024,1024]{1,0:T(8,128)(2,1)} %bitcast.15, bf16[1024,1024]{1,0:T(8,128)(2,1)} %bitcast.16), custom_call_target="tpu_custom_call" | custom-call | tf_op jit(solution)/shard_map/block/pallas_call | solution.py:728
  87.7 165.8 %grad_rs.1 = (f32[1024,128]{1,0:T(8,128)}, f32[2,8,128]{2,1,0:T(8,128)}, f32[4,4,4,1024,128]{4,3,2,1,0:T(8,128)}) custom-call(bf16[1024,1024]{1,0:T(8,128)(2,1)} %get-tuple-element.17.x_ref, bf16[1024,4096]{1,0:T(8,128)(2,1)} %get-tuple-element.18.du_ref, bf16[1024,4096]{1,0:T(8,128)(2,1)} %get-tuple-element.19.a_ref, ...), custom_call_target="tpu_custom_call" | custom-call | tf_op jit(solution)/shard_map/grad_rs/pallas_call | solution.py:375
  253.6 3.7 %adam.1 = (f32[1024,128]{1,0:T(8,128)}, f32[1024,128]{1,0:T(8,128)}, f32[1024,128]{1,0:T(8,128)}, bf16[1024,128]{1,0:T(8,128)(2,1)}, f32[1,1]{1,0:T(1,128)}) custom-call(f32[1024,128]{1,0:T(8,128)} %get-tuple-element.22.part_ref, f32[2,8,128]{2,1,0:T(8,128)} %get-tuple-element.23.total_ref, f32[1,1]{1,0:T(1,128)} %bitcast.12.tau_ref, f32[1024,128]{1,0:T(8,128)} %bitcast.17, ...), custom_call_target="tpu_custom_call" | custom-call | tf_op jit(solution)/shard_map/adam/pallas_call | solution.py:774
  257.3 0.0 copy-start
  257.3 0.9 copy-done
  258.3 74.5 %weight_ag.1 = f32[4,4,4,1024,128]{4,3,2,1,0:T(8,128)} custom-call(bf16[1024,128]{1,0:T(8,128)(2,1)S(1)} %copy-done), custom_call_target="tpu_custom_call" | custom-call | tf_op jit(solution)/shard_map/weight_ag/pallas_call | solution.py:511
  332.8 26.4 %convert_element_type.3 = bf16[1,1,8388608]{2,1,0:T(2,128)(2,1)} convert(f32[1,1,8388608]{2,1,0:T(1,128)} %bitcast.13) | non-fusion elementwise | flops 8388608 | bytes 50331648 | tf_op jit(solution)/shard_map/convert_element_type | solution.py:794
Async XLA Ops:
  257.3 0.9 copy-start

commit v4 on v3

--- a/solution.py
+++ b/solution.py
@@ -16,8 +16,8 @@
 MESH = pl.DeviceIdType.MESH
 MIB = 1024 * 1024
 
-SUBS = 4
-SUB_ROWS = 256
+UNITS = (1, 2, 2, 2, 1)
+SUBS = len(UNITS)
 ALL = slice(None)
 RING = pl.ds(0, 4)
 BOTH = range(2)
@@ -37,9 +37,8 @@
 LANES = 128
 STEPS = ROWS // TILE
 PIECE = 131072
-CHUNK = 4 * PIECE
-CHUNKS = 2 * ROWS * WIDE // CHUNK
-SLOTS = 4
+CHUNKS = 2 * ROWS * WIDE // PIECE
+SLOTS = 16
 PITCH = 40
 GELU_A = math.sqrt(2.0 / math.pi)
 GELU_B = GELU_A * 0.044715
@@ -60,17 +59,19 @@
 
 
 def rs_split():
-    table = {}
-    for s in range(SUBS):
-        sizes = [11, 11, 11]
-        sizes[(s + 2) % 3] = 10
-        start = 32 * s
+    table, half_at, full_at = {}, [0], [0]
+    start = 0
+    for s, units in enumerate(UNITS):
+        most = 0
         for c in AXES:
-            n = sizes[c]
+            n = (16 * units + (c + s) % 3) // 3
             first = (n + (s + c) % 2) // 2
             table[s, c] = tuple(8 * k for k in (start, first, n - first))
             start += n
-    return table
+            most = max(most, n)
+        half_at.append(half_at[s] + (most + 1) // 2 * 8)
+        full_at.append(full_at[s] + most * 8)
+    return table, half_at, full_at
 
 
 def coords_of(me):
@@ -122,7 +123,7 @@
 def rs_kernel(x_ref, du_ref, a_ref, top_ref, loss_ref, out_ref, total_ref, g_ref, ra1, rb1, lb, own, ra2, rb2, ra3, rb3, ssem, rsem, lsem,
               acc, got, tsem, usem, xb, gb, dub, ab, put1, put2, insem, dusem, asem, psem1, psem2):
     coords = coords_of(lax.axis_index("data"))
-    table = rs_split()
+    table, half_at, full_at = rs_split()
     ra = (ra1, ra2, ra3)
     rb = (rb1, rb2, rb3)
     copies = {}
@@ -131,13 +132,16 @@
     load_g = pltpu.make_async_copy(top_ref, gb, insem.at[1])
 
     def load_du(s):
-        return pltpu.make_async_copy(du_ref.at[:, pl.ds(s * ROWS, ROWS)], dub.at[s % 2], dusem.at[s % 2])
+        width = UNITS[s] * COLS
+        return pltpu.make_async_copy(du_ref.at[:, pl.ds(sum(UNITS[:s]) * COLS, width)], dub.at[s % 2, :, upto(width)], dusem.at[s % 2])
 
     def load_a(m):
         return pltpu.make_async_copy(a_ref.at[:, pl.ds(pl.multiple_of(m * COLS, COLS), COLS)], ab.at[lax.rem(m, 2)], asem.at[lax.rem(m, 2)])
 
     def grads(s):
-        band = pl.ds(s * SUB_ROWS, SUB_ROWS)
+        size = UNITS[s] * LANES
+        band = pl.ds(sum(UNITS[:s]) * LANES, size)
+        width = UNITS[s] * COLS
         load_a(0).start()
         if s + 1 < SUBS:
             load_du(s + 1).start()
@@ -147,21 +151,21 @@
             load_g.wait()
 
         def write1(m):
-            return pltpu.make_async_copy(put1.at[lax.rem(m, 2)], g_ref.at[m // 2, pl.ds(lax.rem(m, 2) * 2, 2), :, band, :],
+            return pltpu.make_async_copy(put1.at[lax.rem(m, 2), :, :, upto(size)], g_ref.at[m // 2, pl.ds(lax.rem(m, 2) * 2, 2), :, band, :],
                                          psem1.at[lax.rem(m, 2)])
 
         def write2(m):
-            return pltpu.make_async_copy(put2.at[lax.rem(m, 2)], g_ref.at[m // 4 + 2, lax.rem(m, 4), :, band, :],
+            return pltpu.make_async_copy(put2.at[lax.rem(m, 2), :, upto(size)], g_ref.at[m // 4 + 2, lax.rem(m, 4), :, band, :],
                                          psem2.at[lax.rem(m, 2)])
 
         def first(m, carry):
-            val = dot32(xb[:, pl.ds(pl.multiple_of(m * TILE, TILE), TILE)], dub[s % 2], ROWWISE)
+            val = dot32(xb[:, pl.ds(pl.multiple_of(m * TILE, TILE), TILE)], dub[s % 2, :, upto(width)], ROWWISE)
 
             @pl.when(m > 1)
             def _():
                 write1(m - 2).wait()
 
-            for ct in range(ROWS // LANES):
+            for ct in range(width // LANES):
                 put1[lax.rem(m, 2), :, :, ct * 32:(ct + 1) * 32, :] = val[:, ct * LANES:(ct + 1) * LANES].reshape(2, 4, 32, LANES)
             write1(m).start()
             return carry
@@ -179,7 +183,7 @@
             def _():
                 write2(m - 2).wait()
 
-            for ct in BOTH:
+            for ct in range(UNITS[s]):
                 part = slice(ct * LANES, (ct + 1) * LANES)
                 put2[lax.rem(m, 2), :, part, :] = val[:, part].reshape(4, LANES, LANES)
             write2(m).start()
@@ -222,7 +226,7 @@
             idx = [RING] * 3
             idx[RS_ORDER[c][0]] = k
             return g_ref.at[tuple(idx) + (pl.ds(table[s, c][0] + lo, n), ALL)]
-        return own.at[(s * 3 + c,) + lead(ph, c, k) + (pl.ds(lo, n), ALL)]
+        return own.at[(c,) + lead(ph, c, k) + (pl.ds(full_at[s] + lo, n), ALL)]
 
     def slot(ref, ph, i, lo, n):
         return ref.at[(i,) + (RING,) * (2 - ph) + (pl.ds(lo, n), ALL)]
@@ -241,12 +245,12 @@
     def send_a(ph, s, c):
         for d in BOTH:
             n = rows(s, c, d)[1]
-            start(ph, s, c, d, 0, source(ph, s, c, at(c, ph, 2), d), slot(ra[ph], ph, s * 6 + c * 2 + d, 0, n))
+            start(ph, s, c, d, 0, source(ph, s, c, at(c, ph, 2), d), slot(ra[ph], ph, c * 2 + d, half_at[s], n))
 
     def send_b1(ph, s, c):
         for d in BOTH:
             lo, n = rows(s, c, 1 - d)
-            start(ph, s, c, d, 1, source(ph, s, c, at(c, ph, DELTAS[d]), 1 - d), slot(rb[ph], ph, s * 6 + c * 2 + d, lo, n))
+            start(ph, s, c, d, 1, source(ph, s, c, at(c, ph, DELTAS[d]), 1 - d), slot(rb[ph], ph, c * 2 + d, full_at[s] + lo, n))
 
     def load(s, c):
         for d in BOTH:
@@ -256,13 +260,13 @@
             copy.start()
             copies["lb", s, c, d] = copy
         n = rows(s, c, 2)[1]
-        copy = pltpu.make_async_copy(source(0, s, c, at(c, 0, 0), 2), slot(own, 0, s * 3 + c, 0, n), lsem.at[s * 9 + c * 3 + 2])
+        copy = pltpu.make_async_copy(source(0, s, c, at(c, 0, 0), 2), slot(own, 0, c, full_at[s], n), lsem.at[s * 9 + c * 3 + 2])
         copy.start()
         copies["own", s, c] = copy
 
     def forward(ph, s, c):
         for d in BOTH:
-            i = s * 6 + c * 2 + d
+            i = c * 2 + d
             lo, n = rows(s, c, d)
             if ph == 0:
                 copies["lb", s, c, d].wait()
@@ -272,12 +276,12 @@
 
             def body(t, carry, d=d, i=i, n=n, lo=lo, buf=buf, k=k):
                 where, mine = lead_t(ph, c, k, t)
-                term = lb[(s % 2 * 6 + c * 2 + d,) + where + (upto(n), ALL)] if ph == 0 else own[(s * 3 + c,) + mine + (pl.ds(lo, n), ALL)]
-                buf[(i,) + where + (upto(n), ALL)] += term
+                term = lb[(s % 2 * 6 + c * 2 + d,) + where + (upto(n), ALL)] if ph == 0 else own[(c,) + mine + (pl.ds(full_at[s] + lo, n), ALL)]
+                buf[(i,) + where + (pl.ds(half_at[s], n), ALL)] += term
                 return carry
 
             lax.fori_loop(0, LEADS[ph], body, 0)
-            start(ph, s, c, d, 2, slot(buf, ph, i, 0, n), slot(rb[ph], ph, i, lo, n))
+            start(ph, s, c, d, 2, slot(buf, ph, i, half_at[s], n), slot(rb[ph], ph, i, full_at[s] + lo, n))
 
     def finish(ph, s, c):
         if ph == 0:
@@ -286,14 +290,14 @@
             copies[ph, s, c, d, 1].wait_recv()
             copies[ph, s, c, d, 2].wait_recv()
         n = rows(s, c, 2)[1]
-        i, j = s * 6 + c * 2, s * 3 + c
+        i = c * 2
         buf = rb[ph]
         k = at(c, ph, 0)
-        span = upto(n)
+        span = pl.ds(full_at[s], n)
 
         def body(t, carry):
             where, mine = lead_t(ph, c, k, t)
-            mine = (j,) + mine + (span, ALL)
+            mine = (c,) + mine + (span, ALL)
             total = own[mine] + buf[(i,) + where + (span, ALL)] + buf[(i + 1,) + where + (span, ALL)]
             if ph < 2:
                 own[mine] = total
@@ -332,14 +336,19 @@
         if s < SUBS:
             st0b(s)
 
-    steps = []
+    queue = [(mid, 0), (None, 0), (mid, 1)]
     for s in range(SUBS):
-        done = 3 * s + 4
-        steps.append((max(s, 3 * s - 1), 0, mid, 0, s))
-        for ph in AXES:
-            steps.append((done + 4 * ph, 1, turn, ph, s))
-            if ph:
-                steps.append((done + 4 * ph - 2, 1, mid, ph, s))
+        queue += [(turn, s), (None, s + 1), (mid, s + 2)]
+    steps, clock = [], 0
+    for act, s in queue:
+        if s < SUBS:
+            clock += UNITS[s]
+            steps.append((clock, 0, act, 0, s))
+            if act is turn:
+                for ph in range(1, 3):
+                    steps.append((clock + 3 * ph - 2, 1, mid, ph, s))
+                    steps.append((clock + 3 * ph, 1, turn, ph, s))
+    steps = [e for e in steps if e[2]]
     load_x.start()
     load_du(0).start()
     load_g.start()
@@ -369,8 +378,13 @@
     vmem = pl.BlockSpec(memory_space=pltpu.VMEM)
     anywhere = pl.BlockSpec(memory_space=pl.ANY)
 
-    def slots(n, axes, rows, subs=SUBS):
-        return pltpu.VMEM((subs * n,) + (4,) * axes + (rows, LANES), f32)
+    _, half_at, full_at = rs_split()
+
+    def slots(n, axes, rows):
+        return pltpu.VMEM((n,) + (4,) * axes + (rows, LANES), f32)
+
+    def landing(axes):
+        return [slots(6, axes, half_at[-1]), slots(6, axes, full_at[-1])]
 
     part, totals, _ = pl.pallas_call(
         rs_kernel,
@@ -378,12 +392,12 @@
                    jax.ShapeDtypeStruct((4, 4, 4, ROWS, LANES), f32)),
         in_specs=[anywhere] * 4 + [vmem],
         out_specs=(vmem, vmem, anywhere),
-        scratch_shapes=[slots(6, 2, 48), slots(6, 2, 88), slots(6, 2, 48, 2), slots(3, 2, 88), slots(6, 1, 48), slots(6, 1, 88),
-                        slots(6, 0, 48), slots(6, 0, 88), dma((sems,)), dma((sems,)), dma((SUBS * 9,)),
+        scratch_shapes=[*landing(2), slots(12, 2, 48), slots(3, 2, full_at[-1]), *landing(1), *landing(0),
+                        dma((sems,)), dma((sems,)), dma((SUBS * 9,)),
                         pltpu.VMEM((5, 2, 8, LANES), f32), pltpu.VMEM((4, 4, 2, 8, LANES), f32), dma((10,)), dma((10,)),
                         pltpu.VMEM((ROWS, ROWS), BF16), pltpu.VMEM((ROWS, ROWS), BF16), pltpu.VMEM((2, ROWS, ROWS), BF16),
-                        pltpu.VMEM((2, ROWS, COLS), BF16), pltpu.VMEM((2, 2, 4, SUB_ROWS, LANES), f32),
-                        pltpu.VMEM((2, 4, SUB_ROWS, LANES), f32), dma((2,)), dma((2,)), dma((2,)), dma((2,)), dma((2,))],
+                        pltpu.VMEM((2, ROWS, COLS), BF16), pltpu.VMEM((2, 2, 4, TILE, LANES), f32),
+                        pltpu.VMEM((2, 4, TILE, LANES), f32), dma((2,)), dma((2,)), dma((2,)), dma((2,)), dma((2,))],
         compiler_params=pltpu.CompilerParams(collective_id=0, has_side_effects=True, vmem_limit_bytes=63 * MIB),
         name="grad_rs",
     )(x, du, a, g, loss)
@@ -400,7 +414,7 @@
     return table
 
 
-def ag_kernel(w_ref, wide_ref, out_ref, stage, ssem, rsem, lsem):
+def ag_kernel(w_ref, wide_ref, out_ref, ssem, rsem):
     coords = coords_of(lax.axis_index("data"))
     table = ag_split()
     copies = {}
@@ -451,31 +465,24 @@
             for d in BOTH:
                 copies[c, unit, d, piece].wait_recv()
 
-    flights = []
-
-    def widen(unit):
-        for c in AXES:
-            start, n0, n1 = table[c]
-            n = n0 + n1
-            second = AG_ORDER[c][1]
-            q = wrap(coords[second] + UNIT_SHIFT[unit])
-            i = len(flights)
-            if i > 1:
-                flights[i - 2].wait()
-
-            def body(t, carry):
-                u, v = divide(t)
-                where = [u, v]
-                where.insert(second, q)
-                stage[i % 2, u, v, upto(n), :] = out_ref[tuple(where) + (pl.ds(start, n), ALL)].astype(jnp.float32)
-                return carry
-
-            lax.fori_loop(0, 16, body, 0)
-            where = [RING] * 2
-            where.insert(second, q)
-            flights.append(pltpu.make_async_copy(stage.at[i % 2, :, :, upto(n), :],
-                                                 wide_ref.at[tuple(where) + (pl.ds(start, n), ALL)], lsem.at[i]))
-            flights[i].start()
+    def pack(unit, *shifts):
+        for shift in shifts:
+            for c in AXES:
+                start, n0, n1 = table[c]
+                _, second, third = AG_ORDER[c]
+                at = {second: wrap(coords[second] + UNIT_SHIFT[unit]), third: wrap(coords[third] + shift)}
+
+                def body(t, carry, at=at, start=start, n=n0 + n1):
+                    where = tuple(at.get(p, t) for p in AXES)
+                    z, y, x = where
+                    base = (z * 16 + y * 4 + x) * PIECE + start * LANES
+                    for k in range(n // 16):
+                        line = out_ref[where + (pl.ds(start + k * 16, 16), ALL)].astype(F32)
+                        line = line.reshape(1, 2 * ROWS).astype(BF16)
+                        wide_ref[:, pl.ds(pl.multiple_of(base + k * 2 * ROWS, 2 * ROWS), 2 * ROWS)] = line
+                    return carry
+
+                lax.fori_loop(0, 4, body, 0)
 
     greet(coords, DELTAS, False)
     begin(0)
@@ -485,22 +492,24 @@
     arrive(0, 2)
     begin(1)
     begin(2)
+    pack(2, 0)
     middle(1)
     arrive(1, 1)
     begin(3)
     begin(4)
     middle(2)
+    pack(3, 0)
+    pack(4, 0)
     arrive(1, 2)
     begin(5)
-    middle(3)
-    middle(4)
-    middle(5)
+    pack(5, 0)
     for unit in UNIT_SHIFT:
+        if unit + 1 in UNIT_SHIFT:
+            middle(unit + 1)
         arrive(unit, 1)
+        pack(unit, *DELTAS)
         arrive(unit, 2)
-        widen(unit)
-    for flight in flights[-2:]:
-        flight.wait()
+        pack(unit, 2)
     for copy in copies.values():
         copy.wait_send()
 
@@ -510,12 +519,11 @@
     sems = 36 * 3
     return pl.pallas_call(
         ag_kernel,
-        out_shape=jax.ShapeDtypeStruct((4, 4, 4, 1024, 128), jnp.float32),
+        out_shape=pltpu.VMEM((1, 64 * w.size), BF16),
         in_specs=[pl.BlockSpec(memory_space=pltpu.VMEM)],
-        out_specs=pl.BlockSpec(memory_space=pl.ANY),
-        scratch_shapes=[pltpu.VMEM((4, 4, 4, 1024, 128), w.dtype), pltpu.VMEM((2, 4, 4, 352, 128), jnp.float32),
-                        dma((sems,)), dma((sems,)), dma((12,))],
-        compiler_params=pltpu.CompilerParams(collective_id=1, has_side_effects=True, vmem_limit_bytes=40 * MIB),
+        out_specs=pl.BlockSpec(memory_space=pltpu.VMEM),
+        scratch_shapes=[pltpu.VMEM((4, 4, 4, ROWS, LANES), w.dtype), dma((sems,)), dma((sems,))],
+        compiler_params=pltpu.CompilerParams(collective_id=1, has_side_effects=True, vmem_limit_bytes=24 * MIB),
         name="weight_ag",
     )(w)
 
@@ -536,7 +544,7 @@
     other = {"stage": 1 - stage}
 
     def chunk(i):
-        return pltpu.make_async_copy(w_ref.at[:, pl.ds(pl.multiple_of(i * CHUNK, CHUNK), CHUNK)], raw.at[lax.rem(i, SLOTS)],
+        return pltpu.make_async_copy(w_ref.at[:, pl.ds(pl.multiple_of(i * PIECE, PIECE), PIECE)], raw.at[lax.rem(i, SLOTS)],
                                      wsem.at[lax.rem(i, SLOTS)])
 
     load_x = pltpu.make_async_copy(xin_ref, xb, insem.at[0])
@@ -564,17 +572,14 @@
         rows = PIECE // (blocks * LANES)
         chunk(i).wait()
 
-        def body(q, carry):
-            for j in range(PIECE // ROWS):
-                line = raw[lax.rem(i, SLOTS), :, pl.ds(pl.multiple_of(q * PIECE + j * ROWS, ROWS), ROWS)]
-                at = (j * 8 // blocks) * pitch + j * 8 % blocks
-                wide[at:at + 8, :] = line.astype(F32).reshape(8, LANES)
-            base = pl.ds(pl.multiple_of((lax.rem(i, CHUNKS // 2) * 4 + q) * rows, rows), rows)
-            for cb in range(blocks):
-                weight[base, cb * LANES:(cb + 1) * LANES] = wide[pl.ds(cb, rows, stride=pitch), :].astype(BF16)
-            return carry
-
-        lax.fori_loop(0, 4, body, 0)
+        slot = lax.rem(i, SLOTS)
+        for j in range(PIECE // ROWS):
+            line = raw[slot, :, j * ROWS:(j + 1) * ROWS]
+            at = (j * 8 // blocks) * pitch + j * 8 % blocks
+            wide[at:at + 8, :] = line.astype(F32).reshape(8, LANES)
+        base = pl.ds(pl.multiple_of(lax.rem(i, CHUNKS // 2) * rows, rows), rows)
+        for cb in range(blocks):
+            weight[cb, base, :] = wide[pl.ds(cb, rows, stride=pitch), :].astype(BF16)
 
         @pl.when(i < CHUNKS - SLOTS)
         def _():
@@ -605,6 +610,12 @@
     def cols(j):
         return pl.ds(pl.multiple_of(j * COLS, COLS), COLS)
 
+    def blocks(j):
+        return [j * (COLS // LANES) + q for q in range(COLS // LANES)]
+
+    def beside(weight, which, part):
+        return jnp.concatenate([weight[cb, part, :] for cb in which], axis=1)
+
     def send_h(i):
         return pltpu.make_async_remote_copy(src_ref=hb.at[span(i)], dst_ref=xb.at[span(i)], send_sem=hs.at[i], recv_sem=hr.at[i],
                                             device_id=other, device_id_type=MESH)
@@ -619,7 +630,7 @@
 
     def forward(i):
         def up(j, carry):
-            u = dot32(xb[span(i), :], w1[:, cols(j)]).astype(BF16)
+            u = dot32(xb[span(i), :], beside(w1, blocks(j), ALL)).astype(BF16)
             db[span(i), cols(j)] = u
             uf = u.astype(F32)
             half = 0.5 * uf
@@ -627,7 +638,7 @@
             return carry
 
         def down(j, carry):
-            hb[span(i), cols(j)] = (xb[span(i), cols(j)].astype(F32) + dot32(ab[span(i), :], w2[:, cols(j)])).astype(BF16)
+            hb[span(i), cols(j)] = (xb[span(i), cols(j)].astype(F32) + dot32(ab[span(i), :], beside(w2, blocks(j), ALL))).astype(BF16)
             return carry
 
         lax.fori_loop(0, WIDE // COLS, up, 0, unroll=2)
@@ -641,7 +652,7 @@
 
     def backward(i):
         def body(j, carry):
-            e = dot_t(gb[span(i), :], w2[cols(j), :])
+            e = dot_t(gb[span(i), :], beside(w2, range(ROWS // LANES), cols(j)))
             u = db[span(i), cols(j)].astype(F32)
             sq = u * u
             gate = 0.5 + 0.5 * jnp.tanh(u * (GELU_A + GELU_B * sq))
@@ -653,7 +664,7 @@
 
     def below(i):
         def body(j, carry):
-            hb[span(i), cols(j)] = (gb[span(i), cols(j)].astype(F32) + dot_t(db[span(i), :], w1[cols(j), :])).astype(BF16)
+            hb[span(i), cols(j)] = (gb[span(i), cols(j)].astype(F32) + dot_t(db[span(i), :], beside(w1, range(WIDE // LANES), cols(j)))).astype(BF16)
             return carry
 
         lax.fori_loop(0, ROWS // COLS, body, 0)
@@ -730,8 +741,8 @@
         out_shape=(shape(narrow), shape(wide), shape(wide), shape(narrow), jax.ShapeDtypeStruct((8, LANES), F32)),
         in_specs=[anywhere] * 3,
         out_specs=(anywhere,) * 4 + (pl.BlockSpec(memory_space=pltpu.VMEM),),
-        scratch_shapes=[room(wide), room((WIDE, ROWS)), room(narrow), room(narrow), room(narrow), room(wide), room(wide), room(narrow),
-                        room((SLOTS, 1, CHUNK)), pltpu.VMEM((32 * PITCH, LANES), F32),
+        scratch_shapes=[room((WIDE // LANES, ROWS, LANES)), room((ROWS // LANES, WIDE, LANES)), room(narrow), room(narrow), room(narrow), room(wide), room(wide), room(narrow),
+                        room((SLOTS, 1, PIECE)), pltpu.VMEM((32 * PITCH, LANES), F32),
                         dma((SLOTS,)), dma((2,)), dma((STEPS * 4,)), dma((STEPS,)), dma((STEPS,)), dma((STEPS,)), dma((STEPS,))],
         compiler_params=pltpu.CompilerParams(collective_id=2, has_side_effects=True, vmem_limit_bytes=60 * MIB),
         name="block",
@@ -791,7 +802,7 @@
         rate = LR_BASE / math.sqrt(x_in.shape[-1])
         state = [z.reshape(ROWS, LANES) for z in (w_master, m_prior, v_prior)]
         w_new, m_new, v_new, w_bf, loss_mean = adam(rate, token_count, part, totals, clip_tau.reshape(1, 1), *state)
-        w_all = lax.optimization_barrier(all_gather_rows(w_bf).reshape(w_work.shape)).astype(BF16)
+        w_all = all_gather_rows(w_bf).reshape(w_work.shape)
         return (loss_mean.reshape(()), w_all) + tuple(z.reshape(w_master.shape) for z in (w_new, m_new, v_new))
 
     row_spec = P(None, 'data', None)

time: 360 us -> 360 us (level)
  other arithmetic: 26.4 us -> 0 us
  Pallas kernels: 331 us -> 346 us
  local copies, waits for them, and re-layouts: 0.95 us -> 11.7 us
    convert_element_type x1 -> x0, other arithmetic: 26.4 us -> none  [device_step(): lax.optimization_barrier(all_gather_rows(w_bf).reshape(w_work.shape))]
    pallas_call x1, Pallas kernels: 166 us -> 184 us  [reduce_scatter(): pl.pallas_call(rs_kernel, out_shape=(jax.ShapeDtypeStruct((ROWS, LANES),...]
    unnamed x2 -> x1, local copies, waits for them, and re-layouts: 0.95 us -> 11.7 us
    pallas_call x1, Pallas kernels: 86.5 us -> 81 us  [block_passes(): pl.pallas_call(functools.partial(block_kernel, 1.0 / token_count), out_sh...]
where the time goes in v4:
time: 360 us; the launch traced here: 359 us
  Pallas kernels  346 us (96%)
  local copies, waits for them, and re-layouts  11.7 us (3%)
    pallas_call x1, Pallas kernels, reduce_scatter(): pl.pallas_call(rs_kernel, out_shape=(jax.ShapeDtypeStruct((ROWS, LANES),...  184 us
    pallas_call x1, Pallas kernels, block_passes(): pl.pallas_call(functools.partial(block_kernel, 1.0 / token_count), out_sh...  81 us
    pallas_call x1, Pallas kernels, all_gather_rows(): pl.pallas_call(ag_kernel, out_shape=pltpu.VMEM((1, 64 * w.size), BF16), i...  77.1 us
    unnamed x1, local copies, waits for them, and re-layouts  11.7 us

profile of v4, /device:TPU:0, one launch (start us, length us, event | category | flops | bytes accessed | tf_op | source)
XLA Modules:
  0.0 358.8 jit_solution(12159571063342426815)
XLA Ops:
  1.3 81.0 %block.1 = (bf16[1024,1024]{1,0:T(8,128)(2,1)}, bf16[1024,4096]{1,0:T(8,128)(2,1)}, bf16[1024,4096]{1,0:T(8,128)(2,1)}, bf16[1024,1024]{1,0:T(8,128)(2,1)}, f32[8,128]{1,0:T(8,128)}) custom-call(bf16[1,8388608]{1,0:T(2,128)(2,1)} %bitcast.14, bf16[1024,1024]{1,0:T(8,128)(2,1)} %bitcast.15, bf16[1024,1024]{1,0:T(8,128)(2,1)} %bitcast.16), custom_call_target="tpu_custom_call" | custom-call | tf_op jit(solution)/shard_map/block/pallas_call | solution.py:739
  82.3 184.1 %grad_rs.1 = (f32[1024,128]{1,0:T(8,128)}, f32[2,8,128]{2,1,0:T(8,128)}, f32[4,4,4,1024,128]{4,3,2,1,0:T(8,128)}) custom-call(bf16[1024,1024]{1,0:T(8,128)(2,1)} %get-tuple-element.17.x_ref, bf16[1024,4096]{1,0:T(8,128)(2,1)} %get-tuple-element.18.du_ref, bf16[1024,4096]{1,0:T(8,128)(2,1)} %get-tuple-element.19.a_ref, ...), custom_call_target="tpu_custom_call" | custom-call | tf_op jit(solution)/shard_map/grad_rs/pallas_call | solution.py:389
  266.3 3.7 %adam.1 = (f32[1024,128]{1,0:T(8,128)}, f32[1024,128]{1,0:T(8,128)}, f32[1024,128]{1,0:T(8,128)}, bf16[1024,128]{1,0:T(8,128)(2,1)}, f32[1,1]{1,0:T(1,128)}) custom-call(f32[1024,128]{1,0:T(8,128)} %get-tuple-element.22.part_ref, f32[2,8,128]{2,1,0:T(8,128)} %get-tuple-element.23.total_ref, f32[1,1]{1,0:T(1,128)} %bitcast.12.tau_ref, f32[1024,128]{1,0:T(8,128)} %bitcast.17, ...), custom_call_target="tpu_custom_call" | custom-call | tf_op jit(solution)/shard_map/adam/pallas_call | solution.py:785
  270.1 77.1 %weight_ag.1 = bf16[1,8388608]{1,0:T(2,128)(2,1)S(1)} custom-call(bf16[1024,128]{1,0:T(8,128)(2,1)} %get-tuple-element.25.w_ref), custom_call_target="tpu_custom_call" | custom-call | tf_op jit(solution)/shard_map/weight_ag/pallas_call | solution.py:520
  347.1 11.7 %copy.13 = bf16[1,1,8388608]{2,1,0:T(2,128)(2,1)} copy(bf16[1,1,8388608]{2,1,0:T(2,128)(2,1)S(1)} %bitcast.13) | data formatting | bytes 33554432

commit v5 on v4

--- a/solution.py
+++ b/solution.py
@@ -17,6 +17,7 @@
 MIB = 1024 * 1024
 
 UNITS = (1, 2, 2, 2, 1)
+DELAY = 30
 SUBS = len(UNITS)
 ALL = slice(None)
 RING = pl.ds(0, 4)
@@ -346,8 +347,8 @@
             steps.append((clock, 0, act, 0, s))
             if act is turn:
                 for ph in range(1, 3):
-                    steps.append((clock + 3 * ph - 2, 1, mid, ph, s))
-                    steps.append((clock + 3 * ph, 1, turn, ph, s))
+                    steps.append((clock + DELAY * ph - DELAY // 2, 1, mid, ph, s))
+                    steps.append((clock + DELAY * ph, 1, turn, ph, s))
     steps = [e for e in steps if e[2]]
     load_x.start()
     load_du(0).start()

time: 360 us -> 345 us (0.958)
  Pallas kernels: 346 us -> 330 us
    pallas_call x1, Pallas kernels: 184 us -> 169 us  [reduce_scatter(): pl.pallas_call(rs_kernel, out_shape=(jax.ShapeDtypeStruct((ROWS, LANES),...]
where the time goes in v5:
time: 345 us; the launch traced here: 343 us
  Pallas kernels  330 us (96%)
  local copies, waits for them, and re-layouts  11.7 us (3%)
    pallas_call x1, Pallas kernels, reduce_scatter(): pl.pallas_call(rs_kernel, out_shape=(jax.ShapeDtypeStruct((ROWS, LANES),...  169 us
    pallas_call x1, Pallas kernels, block_passes(): pl.pallas_call(functools.partial(block_kernel, 1.0 / token_count), out_sh...  81 us
    pallas_call x1, Pallas kernels, all_gather_rows(): pl.pallas_call(ag_kernel, out_shape=pltpu.VMEM((1, 64 * w.size), BF16), i...  76.6 us
    unnamed x1, local copies, waits for them, and re-layouts  11.7 us

profile of v5, /device:TPU:0, one launch (start us, length us, event | category | flops | bytes accessed | tf_op | source)
XLA Modules:
  0.0 343.4 jit_solution(2043363391111738030)
XLA Ops:
  1.3 81.0 %block.1 = (bf16[1024,1024]{1,0:T(8,128)(2,1)}, bf16[1024,4096]{1,0:T(8,128)(2,1)}, bf16[1024,4096]{1,0:T(8,128)(2,1)}, bf16[1024,1024]{1,0:T(8,128)(2,1)}, f32[8,128]{1,0:T(8,128)}) custom-call(bf16[1,8388608]{1,0:T(2,128)(2,1)} %bitcast.14, bf16[1024,1024]{1,0:T(8,128)(2,1)} %bitcast.15, bf16[1024,1024]{1,0:T(8,128)(2,1)} %bitcast.16), custom_call_target="tpu_custom_call" | custom-call | tf_op jit(solution)/shard_map/block/pallas_call | solution.py:740
  82.3 169.1 %grad_rs.1 = (f32[1024,128]{1,0:T(8,128)}, f32[2,8,128]{2,1,0:T(8,128)}, f32[4,4,4,1024,128]{4,3,2,1,0:T(8,128)}) custom-call(bf16[1024,1024]{1,0:T(8,128)(2,1)} %get-tuple-element.17.x_ref, bf16[1024,4096]{1,0:T(8,128)(2,1)} %get-tuple-element.18.du_ref, bf16[1024,4096]{1,0:T(8,128)(2,1)} %get-tuple-element.19.a_ref, ...), custom_call_target="tpu_custom_call" | custom-call | tf_op jit(solution)/shard_map/grad_rs/pallas_call | solution.py:390
  251.3 3.7 %adam.1 = (f32[1024,128]{1,0:T(8,128)}, f32[1024,128]{1,0:T(8,128)}, f32[1024,128]{1,0:T(8,128)}, bf16[1024,128]{1,0:T(8,128)(2,1)}, f32[1,1]{1,0:T(1,128)}) custom-call(f32[1024,128]{1,0:T(8,128)} %get-tuple-element.22.part_ref, f32[2,8,128]{2,1,0:T(8,128)} %get-tuple-element.23.total_ref, f32[1,1]{1,0:T(1,128)} %bitcast.12.tau_ref, f32[1024,128]{1,0:T(8,128)} %bitcast.17, ...), custom_call_target="tpu_custom_call" | custom-call | tf_op jit(solution)/shard_map/adam/pallas_call | solution.py:786
  255.1 76.6 %weight_ag.1 = bf16[1,8388608]{1,0:T(2,128)(2,1)S(1)} custom-call(bf16[1024,128]{1,0:T(8,128)(2,1)} %get-tuple-element.25.w_ref), custom_call_target="tpu_custom_call" | custom-call | tf_op jit(solution)/shard_map/weight_ag/pallas_call | solution.py:521
  331.7 11.7 %copy.13 = bf16[1,1,8388608]{2,1,0:T(2,128)(2,1)} copy(bf16[1,1,8388608]{2,1,0:T(2,128)(2,1)S(1)} %bitcast.13) | data formatting | bytes 33554432

commit v6 on v5

--- a/solution.py
+++ b/solution.py
@@ -18,6 +18,7 @@
 
 UNITS = (1, 2, 2, 2, 1)
 DELAY = 30
+DEPTH = 4
 SUBS = len(UNITS)
 ALL = slice(None)
 RING = pl.ds(0, 4)
@@ -134,18 +135,22 @@
 
     def load_du(s):
         width = UNITS[s] * COLS
-        return pltpu.make_async_copy(du_ref.at[:, pl.ds(sum(UNITS[:s]) * COLS, width)], dub.at[s % 2, :, upto(width)], dusem.at[s % 2])
+        return pltpu.make_async_copy(du_ref.at[:, pl.ds(sum(UNITS[:s]) * COLS, width)], dub.at[:, upto(width)], dusem)
 
     def load_a(m):
-        return pltpu.make_async_copy(a_ref.at[:, pl.ds(pl.multiple_of(m * COLS, COLS), COLS)], ab.at[lax.rem(m, 2)], asem.at[lax.rem(m, 2)])
+        return pltpu.make_async_copy(a_ref.at[:, pl.ds(pl.multiple_of(m * COLS, COLS), COLS)], ab.at[lax.rem(m, DEPTH)],
+                                     asem.at[lax.rem(m, DEPTH)])
+
+    def first_blocks():
+        for m in range(DEPTH - 1):
+            load_a(m).start()
 
     def grads(s):
         size = UNITS[s] * LANES
         band = pl.ds(sum(UNITS[:s]) * LANES, size)
         width = UNITS[s] * COLS
-        load_a(0).start()
-        if s + 1 < SUBS:
-            load_du(s + 1).start()
+        if s:
+            first_blocks()
         load_du(s).wait()
         if s == 0:
             load_x.wait()
@@ -156,11 +161,11 @@
                                          psem1.at[lax.rem(m, 2)])
 
         def write2(m):
-            return pltpu.make_async_copy(put2.at[lax.rem(m, 2), :, upto(size)], g_ref.at[m // 4 + 2, lax.rem(m, 4), :, band, :],
-                                         psem2.at[lax.rem(m, 2)])
+            return pltpu.make_async_copy(put2.at[lax.rem(m, DEPTH), :, upto(size)], g_ref.at[m // 4 + 2, lax.rem(m, 4), :, band, :],
+                                         psem2.at[lax.rem(m, DEPTH)])
 
         def first(m, carry):
-            val = dot32(xb[:, pl.ds(pl.multiple_of(m * TILE, TILE), TILE)], dub[s % 2, :, upto(width)], ROWWISE)
+            val = dot32(xb[:, pl.ds(pl.multiple_of(m * TILE, TILE), TILE)], dub[:, upto(width)], ROWWISE)
 
             @pl.when(m > 1)
             def _():
@@ -174,27 +179,30 @@
         def second(m, carry):
             load_a(m).wait()
 
-            @pl.when(m < 7)
+            @pl.when(m < WIDE // COLS - DEPTH + 1)
             def _():
-                load_a(m + 1).start()
-
-            val = dot32(ab[lax.rem(m, 2)], gb[:, band], ROWWISE)
-
-            @pl.when(m > 1)
+                load_a(m + DEPTH - 1).start()
+
+            val = dot32(ab[lax.rem(m, DEPTH)], gb[:, band], ROWWISE)
+
+            @pl.when(m >= DEPTH)
             def _():
-                write2(m - 2).wait()
+                write2(m - DEPTH).wait()
 
             for ct in range(UNITS[s]):
                 part = slice(ct * LANES, (ct + 1) * LANES)
-                put2[lax.rem(m, 2), :, part, :] = val[:, part].reshape(4, LANES, LANES)
+                put2[lax.rem(m, DEPTH), :, part, :] = val[:, part].reshape(4, LANES, LANES)
             write2(m).start()
             return carry
 
         lax.fori_loop(0, 4, first, 0)
-        lax.fori_loop(0, 8, second, 0)
+        if s + 1 < SUBS:
+            load_du(s + 1).start()
+        lax.fori_loop(0, WIDE // COLS, second, 0)
         for m in BOTH:
             write1(m + 2).wait()
-            write2(m + 6).wait()
+        for m in range(DEPTH):
+            write2(m + WIDE // COLS - DEPTH).wait()
 
     def rows(s, c, half):
         start, n0, n1 = table[s, c]
@@ -353,6 +361,7 @@
     load_x.start()
     load_du(0).start()
     load_g.start()
+    first_blocks()
     greet(coords, range(1, 4), True)
     opening(0)
     second(0)
@@ -396,9 +405,9 @@
         scratch_shapes=[*landing(2), slots(12, 2, 48), slots(3, 2, full_at[-1]), *landing(1), *landing(0),
                         dma((sems,)), dma((sems,)), dma((SUBS * 9,)),
                         pltpu.VMEM((5, 2, 8, LANES), f32), pltpu.VMEM((4, 4, 2, 8, LANES), f32), dma((10,)), dma((10,)),
-                        pltpu.VMEM((ROWS, ROWS), BF16), pltpu.VMEM((ROWS, ROWS), BF16), pltpu.VMEM((2, ROWS, ROWS), BF16),
-                        pltpu.VMEM((2, ROWS, COLS), BF16), pltpu.VMEM((2, 2, 4, TILE, LANES), f32),
-                        pltpu.VMEM((2, 4, TILE, LANES), f32), dma((2,)), dma((2,)), dma((2,)), dma((2,)), dma((2,))],
+                        pltpu.VMEM((ROWS, ROWS), BF16), pltpu.VMEM((ROWS, ROWS), BF16), pltpu.VMEM((ROWS, ROWS), BF16),
+                        pltpu.VMEM((DEPTH, ROWS, COLS), BF16), pltpu.VMEM((2, 2, 4, TILE, LANES), f32),
+                        pltpu.VMEM((DEPTH, 4, TILE, LANES), f32), dma((2,)), dma, dma((DEPTH,)), dma((2,)), dma((DEPTH,))],
         compiler_params=pltpu.CompilerParams(collective_id=0, has_side_effects=True, vmem_limit_bytes=63 * MIB),
         name="grad_rs",
     )(x, du, a, g, loss)

time: 345 us -> 335 us (0.971)
  Pallas kernels: 330 us -> 322 us
    pallas_call x1, Pallas kernels: 169 us -> 160 us  [reduce_scatter(): pl.pallas_call(rs_kernel, out_shape=(jax.ShapeDtypeStruct((ROWS, LANES),...]
where the time goes in v6:
time: 335 us
  Pallas kernels  322 us (96%)
  local copies, waits for them, and re-layouts  11.7 us (3%)
    pallas_call x1, Pallas kernels, reduce_scatter(): pl.pallas_call(rs_kernel, out_shape=(jax.ShapeDtypeStruct((ROWS, LANES),...  160 us
    pallas_call x1, Pallas kernels, block_passes(): pl.pallas_call(functools.partial(block_kernel, 1.0 / token_count), out_sh...  81 us
    pallas_call x1, Pallas kernels, all_gather_rows(): pl.pallas_call(ag_kernel, out_shape=pltpu.VMEM((1, 64 * w.size), BF16), i...  77.1 us
    unnamed x1, local copies, waits for them, and re-layouts  11.7 us

profile of v6, /device:TPU:0, one launch (start us, length us, event | category | flops | bytes accessed | tf_op | source)
XLA Modules:
  0.0 335.0 jit_solution(13402469756178263992)
XLA Ops:
  1.3 81.0 %block.1 = (bf16[1024,1024]{1,0:T(8,128)(2,1)}, bf16[1024,4096]{1,0:T(8,128)(2,1)}, bf16[1024,4096]{1,0:T(8,128)(2,1)}, bf16[1024,1024]{1,0:T(8,128)(2,1)}, f32[8,128]{1,0:T(8,128)}) custom-call(bf16[1,8388608]{1,0:T(2,128)(2,1)} %bitcast.14, bf16[1024,1024]{1,0:T(8,128)(2,1)} %bitcast.15, bf16[1024,1024]{1,0:T(8,128)(2,1)} %bitcast.16), custom_call_target="tpu_custom_call" | custom-call | tf_op jit(solution)/shard_map/block/pallas_call | solution.py:749
  82.3 160.3 %grad_rs.1 = (f32[1024,128]{1,0:T(8,128)}, f32[2,8,128]{2,1,0:T(8,128)}, f32[4,4,4,1024,128]{4,3,2,1,0:T(8,128)}) custom-call(bf16[1024,1024]{1,0:T(8,128)(2,1)} %get-tuple-element.17.x_ref, bf16[1024,4096]{1,0:T(8,128)(2,1)} %get-tuple-element.18.du_ref, bf16[1024,4096]{1,0:T(8,128)(2,1)} %get-tuple-element.19.a_ref, ...), custom_call_target="tpu_custom_call" | custom-call | tf_op jit(solution)/shard_map/grad_rs/pallas_call | solution.py:399
  242.6 3.7 %adam.1 = (f32[1024,128]{1,0:T(8,128)}, f32[1024,128]{1,0:T(8,128)}, f32[1024,128]{1,0:T(8,128)}, bf16[1024,128]{1,0:T(8,128)(2,1)}, f32[1,1]{1,0:T(1,128)}) custom-call(f32[1024,128]{1,0:T(8,128)} %get-tuple-element.22.part_ref, f32[2,8,128]{2,1,0:T(8,128)} %get-tuple-element.23.total_ref, f32[1,1]{1,0:T(1,128)} %bitcast.12.tau_ref, f32[1024,128]{1,0:T(8,128)} %bitcast.17, ...), custom_call_target="tpu_custom_call" | custom-call | tf_op jit(solution)/shard_map/adam/pallas_call | solution.py:795
  246.3 77.1 %weight_ag.1 = bf16[1,8388608]{1,0:T(2,128)(2,1)S(1)} custom-call(bf16[1024,128]{1,0:T(8,128)(2,1)} %get-tuple-element.25.w_ref), custom_call_target="tpu_custom_call" | custom-call | tf_op jit(solution)/shard_map/weight_ag/pallas_call | solution.py:530
  323.4 11.7 %copy.13 = bf16[1,1,8388608]{2,1,0:T(2,128)(2,1)} copy(bf16[1,1,8388608]{2,1,0:T(2,128)(2,1)S(1)} %bitcast.13) | data formatting | bytes 33554432

commit v7 on v6

--- a/solution.py
+++ b/solution.py
@@ -514,10 +514,11 @@
     begin(5)
     pack(5, 0)
     for unit in UNIT_SHIFT:
-        if unit + 1 in UNIT_SHIFT:
-            middle(unit + 1)
+        if unit > 2:
+            middle(unit)
         arrive(unit, 1)
         pack(unit, *DELTAS)
+    for unit in UNIT_SHIFT:
         arrive(unit, 2)
         pack(unit, 2)
     for copy in copies.values():
@@ -696,6 +697,9 @@
             def _():
                 send_h(i).start()
 
+            for copy in outputs(i)[:2]:
+                copy.start()
+
             @pl.when(last)
             def _():
                 top(i)
@@ -713,7 +717,7 @@
                 below(i)
                 send_g(i).start()
 
-            for copy in outputs(i):
+            for copy in outputs(i)[2:]:
                 copy.start()
         return carry
 

time: 335 us -> 330 us (0.985)
  Pallas kernels: 322 us -> 316 us
    pallas_call x1, Pallas kernels: 77.1 us -> 72 us  [all_gather_rows(): pl.pallas_call(ag_kernel, out_shape=pltpu.VMEM((1, 64 * w.size), BF16), i...]
where the time goes in v7:
time: 330 us; the launch traced here: 329 us
  Pallas kernels  316 us (96%)
  local copies, waits for them, and re-layouts  11.7 us (4%)
    pallas_call x1, Pallas kernels, reduce_scatter(): pl.pallas_call(rs_kernel, out_shape=(jax.ShapeDtypeStruct((ROWS, LANES),...  160 us
    pallas_call x1, Pallas kernels, block_passes(): pl.pallas_call(functools.partial(block_kernel, 1.0 / token_count), out_sh...  80.2 us
    pallas_call x1, Pallas kernels, all_gather_rows(): pl.pallas_call(ag_kernel, out_shape=pltpu.VMEM((1, 64 * w.size), BF16), i...  72 us
    unnamed x1, local copies, waits for them, and re-layouts  11.7 us

profile of v7, /device:TPU:0, one launch (start us, length us, event | category | flops | bytes accessed | tf_op | source)
XLA Modules:
  0.0 329.3 jit_solution(1946422053564065220)
XLA Ops:
  1.3 80.2 %block.1 = (bf16[1024,1024]{1,0:T(8,128)(2,1)}, bf16[1024,4096]{1,0:T(8,128)(2,1)}, bf16[1024,4096]{1,0:T(8,128)(2,1)}, bf16[1024,1024]{1,0:T(8,128)(2,1)}, f32[8,128]{1,0:T(8,128)}) custom-call(bf16[1,8388608]{1,0:T(2,128)(2,1)} %bitcast.14, bf16[1024,1024]{1,0:T(8,128)(2,1)} %bitcast.15, bf16[1024,1024]{1,0:T(8,128)(2,1)} %bitcast.16), custom_call_target="tpu_custom_call" | custom-call | tf_op jit(solution)/shard_map/block/pallas_call | solution.py:753
  81.5 160.3 %grad_rs.1 = (f32[1024,128]{1,0:T(8,128)}, f32[2,8,128]{2,1,0:T(8,128)}, f32[4,4,4,1024,128]{4,3,2,1,0:T(8,128)}) custom-call(bf16[1024,1024]{1,0:T(8,128)(2,1)} %get-tuple-element.17.x_ref, bf16[1024,4096]{1,0:T(8,128)(2,1)} %get-tuple-element.18.du_ref, bf16[1024,4096]{1,0:T(8,128)(2,1)} %get-tuple-element.19.a_ref, ...), custom_call_target="tpu_custom_call" | custom-call | tf_op jit(solution)/shard_map/grad_rs/pallas_call | solution.py:399
  241.8 3.7 %adam.1 = (f32[1024,128]{1,0:T(8,128)}, f32[1024,128]{1,0:T(8,128)}, f32[1024,128]{1,0:T(8,128)}, bf16[1024,128]{1,0:T(8,128)(2,1)}, f32[1,1]{1,0:T(1,128)}) custom-call(f32[1024,128]{1,0:T(8,128)} %get-tuple-element.22.part_ref, f32[2,8,128]{2,1,0:T(8,128)} %get-tuple-element.23.total_ref, f32[1,1]{1,0:T(1,128)} %bitcast.12.tau_ref, f32[1024,128]{1,0:T(8,128)} %bitcast.17, ...), custom_call_target="tpu_custom_call" | custom-call | tf_op jit(solution)/shard_map/adam/pallas_call | solution.py:799
  245.6 72.0 %weight_ag.1 = bf16[1,8388608]{1,0:T(2,128)(2,1)S(1)} custom-call(bf16[1024,128]{1,0:T(8,128)(2,1)} %get-tuple-element.25.w_ref), custom_call_target="tpu_custom_call" | custom-call | tf_op jit(solution)/shard_map/weight_ag/pallas_call | solution.py:531
  317.6 11.7 %copy.13 = bf16[1,1,8388608]{2,1,0:T(2,128)(2,1)} copy(bf16[1,1,8388608]{2,1,0:T(2,128)(2,1)S(1)} %bitcast.13) | data formatting | bytes 33554432
